TPU v7x, 32 devices: a whole 2x2x4 slice. The times are simulated.
32 devices in a mesh: text: 16 (over z, y, x), query: 2 (over core).
Axes of the slice: x: 2, y: 2, z: 4, core: 2. Of those that a mesh axis runs over, the one named last changes fastest.
Arguments:
- query_embed: bfloat16 [1024, 1024], P(('text', 'query')), may hold values from -6 to 6
- truth_ids: int32 [1024], P(('text', 'query')), may hold values from 0 to 8191
- text_embed: bfloat16 [8192, 1024], P('text'), may hold values from -0.1875 to 0.1875
- text_ids: int32 [8192], P('text'), may hold values from 0 to 8191, each once
Outputs:
- top_scores: float32 [1024, 10], P(('text', 'query'))
- margins: float32 [1024, 3], P(('text', 'query'))
Inputs may be any that keep to these rules, and one draw needn't show every extreme that they name: `text_ids`: every id of 0 to 8191 stands in exactly one row.
All inputs are finite; a program needn't handle non-finite values.
Results may differ from a plain program's by a relative error of at most 0.0003.
Values may be sent and summed in bfloat16 or wider, within the bound.
No kernel may reach another device: no remote copies, remote signals or barrier semaphores. Data moves between devices by JAX's collectives and lax.ppermute only.
A program may use at most 64 MiB of HBM per device.

v0:
```python
import jax
import jax.numpy as jnp
from jax import lax
from jax.experimental import pallas as pl
from jax.experimental.pallas import tpu as pltpu
from jax.sharding import PartitionSpec as P

TOPK = 10
LANES = 128
PLANE = 4
PAIR = 4


def exchange(c, i, j):
    c[i], c[j] = jnp.maximum(c[i], c[j]), jnp.minimum(c[i], c[j])


def sort_pairs(n):
    pairs = []
    p = 1
    while p < n:
        k = p
        while k >= 1:
            for j in range(k % p, n - k, 2 * k):
                for i in range(min(k, n - j - k)):
                    if (i + j) // (2 * p) == (i + j + k) // (2 * p):
                        pairs.append((i + j, i + j + k))
            k //= 2
        p *= 2
    return pairs


def sort_top(values):
    c = list(values)
    for i, j in sort_pairs(len(c)):
        exchange(c, i, j)
    return c[:TOPK]


def merge_top(a, b):
    c = [jnp.maximum(a[i], b[TOPK - 1 - i]) for i in range(TOPK)]
    exchange(c, 0, 8)
    exchange(c, 1, 9)
    head = [jnp.maximum(c[0], c[1]), jnp.minimum(c[0], c[1])]
    tail = [c[8], c[9]] + c[2:8]
    for step in (4, 2, 1):
        for i in range(8):
            if i & step == 0:
                exchange(tail, i, i + step)
    return head + tail


def pack_queries(query_ref, ids_ref, out_ref):
    rows, depth = query_ref.shape
    columns = depth // LANES
    for j in range(columns):
        out_ref[0, j * rows : (j + 1) * rows, :] = query_ref[:, j * LANES : (j + 1) * LANES]
    ids = jnp.concatenate([ids_ref[...], jnp.zeros((1, LANES - rows), jnp.int32)], axis=1)
    high = (ids >> 8).astype(jnp.float32)
    low = (ids & 255).astype(jnp.float32)
    row = lax.broadcasted_iota(jnp.int32, (16, LANES), 0)
    digits = jnp.where(row == 0, high, jnp.where(row == 1, low, 0.0))
    out_ref[0, columns * rows :, :] = digits.astype(jnp.bfloat16)


def pack_texts(core_ref, text_ref, ids_ref, out_ref):
    half, depth = text_ref.shape
    out_ref[:half, :] = text_ref[...]
    row = lax.broadcasted_iota(jnp.int32, (16, half), 0)
    ids = ids_ref[...]
    high = (ids >> 8).astype(jnp.float32)
    low = (ids & 255).astype(jnp.float32)
    digits = jnp.where(row == 0, high, jnp.where(row == 1, low, 0.0))
    out_ref[half:, :half] = digits.astype(jnp.bfloat16)
    out_ref[half:, half:] = jnp.zeros((16, depth - half), jnp.bfloat16)


def scan(text_ref, queries, label_ref, score_ref, wanted, states):
    count = score_ref.shape[0]
    piece = min(count, 2 * LANES)
    for r in range(0, count, piece):
        score_ref[r : r + piece, :] = lax.dot_general(
            text_ref[r : r + piece, :],
            queries,
            (((1,), (1,)), ((), ())),
            preferred_element_type=jnp.float32,
        )
    results = []
    for h, state in enumerate(states):
        lanes = slice(h * LANES, (h + 1) * LANES)

        def step(g, carry):
            best, truth = list(carry[:TOPK]), carry[TOPK]
            values = []
            for i in range(16):
                at = pl.ds(pl.multiple_of(g * LANES + i * 8, 8), 8)
                s = score_ref[at, lanes]
                truth = truth + jnp.where(label_ref[at, :] == wanted[h], s, 0.0)
                values.append(s)
            return tuple(merge_top(best, sort_top(values))) + (truth,)

        results.append(lax.fori_loop(0, count // LANES, step, tuple(state)))
    return results


def spread(row, label_ref):
    for i in range(0, row.shape[1], LANES):
        label_ref[i : i + LANES, :] = jnp.broadcast_to(row[:, i : i + LANES], (LANES, LANES)).T


def joined(digits):
    digits = digits.astype(jnp.float32)
    return digits[0:1] * 256.0 + digits[1:2]


def rank_own(*refs, tiles, rows):
    text_ref, ids_ref = refs[:2]
    bundles = refs[2 : 2 + PLANE]
    query_ref, wanted_ref, state_ref, score_ref, label_ref = refs[2 + PLANE :]
    columns = text_ref.shape[1] // LANES
    spread(ids_ref[...].astype(jnp.float32), label_ref)
    wanted = []
    for h in range(tiles):
        total = jnp.zeros((1, LANES), jnp.float32)
        for d in range(PLANE):
            at = slice(h * LANES + d * rows, h * LANES + (d + 1) * rows)
            for j in range(columns):
                block = bundles[d][h, j * rows : (j + 1) * rows, :]
                query_ref[at, j * LANES : (j + 1) * LANES] = block
            here = joined(bundles[d][h, columns * rows :, :])
            total = total + (here if d == 0 else pltpu.roll(here, d * rows, 1))
        wanted.append(jnp.broadcast_to(total, (8, LANES)))
        wanted_ref[h] = wanted[h]
    low = jnp.full((8, LANES), -jnp.inf, jnp.float32)
    start = [low] * TOPK + [jnp.zeros((8, LANES), jnp.float32)]
    states = scan(text_ref, query_ref[...], label_ref, score_ref, wanted, [start] * tiles)
    for h in range(tiles):
        for i in range(TOPK + 1):
            state_ref[h, i] = states[h][i]


def scan_more(part_ref, query_ref, wanted_ref, state_ref, score_ref, label_ref):
    half = part_ref.shape[0] - 16
    tiles = state_ref.shape[0]
    spread(joined(part_ref[half:, :half]), label_ref)
    wanted = [wanted_ref[h] for h in range(tiles)]
    states = [[state_ref[h, i] for i in range(TOPK + 1)] for h in range(tiles)]
    return scan(part_ref, query_ref[...], label_ref, score_ref, wanted, states)


def rank_near(near_ref, query_ref, wanted_ref, state_ref, next_ref, score_ref, label_ref):
    states = scan_more(near_ref, query_ref, wanted_ref, state_ref, score_ref, label_ref)
    for h, state in enumerate(states):
        for i in range(TOPK + 1):
            next_ref[h, i] = state[i]


def rank_far(far_ref, query_ref, wanted_ref, state_ref, *refs):
    outs, (score_ref, label_ref) = refs[:-2], refs[-2:]
    states = scan_more(far_ref, query_ref, wanted_ref, state_ref, score_ref, label_ref)
    for out_ref, state in zip(outs, states):
        best, truth = list(state[:TOPK]), state[TOPK]
        for shift in (4, 2, 1):
            best = merge_top(best, [pltpu.roll(b, shift, 0) for b in best])
        for i in range(TOPK):
            out_ref[i : i + 1, :] = best[i][0:1, :]
        out_ref[TOPK : TOPK + 1, :] = jnp.sum(truth, axis=0, keepdims=True)
        out_ref[TOPK + 1 :, :] = jnp.zeros((16 - TOPK - 1, LANES), jnp.float32)


def join(ours_ref, theirs_ref, out_ref):
    best = merge_top(
        [ours_ref[i : i + 1, :] for i in range(TOPK)], [theirs_ref[i : i + 1, :] for i in range(TOPK)]
    )
    for i in range(TOPK):
        out_ref[i : i + 1, :] = best[i]
    out_ref[TOPK : TOPK + 1, :] = ours_ref[TOPK : TOPK + 1, :] + theirs_ref[TOPK : TOPK + 1, :]
    out_ref[TOPK + 1 :, :] = jnp.zeros_like(out_ref[TOPK + 1 :, :])


def finish(*refs, rows):
    lists = []
    for d in range(PLANE):
        x = refs[d][...]
        lists.append(x if d == 0 else pltpu.roll(x, LANES - d * rows, 1))
    top_ref, margin_ref = refs[PLANE:]
    ranks = [[x[i : i + 1, :] for i in range(TOPK)] for x in lists]
    best = merge_top(merge_top(ranks[0], ranks[1]), merge_top(ranks[2], ranks[3]))
    truth = lists[0] + lists[1] + lists[2] + lists[3]
    truth = truth[TOPK : TOPK + 1, :]
    for i in range(TOPK):
        top_ref[i : i + 1, :] = best[i][:, :rows]
    for i, k in enumerate((0, 4, 9)):
        margin_ref[i : i + 1, :] = (truth - best[k])[:, :rows]


def kernel(body, out_shape, mib, flops=0, **extra):
    size = sum(x.size * x.dtype.itemsize for x in jax.tree.leaves(out_shape))
    return pl.pallas_call(
        body,
        out_shape=out_shape,
        compiler_params=pltpu.CompilerParams(vmem_limit_bytes=mib << 20),
        cost_estimate=pl.CostEstimate(flops=flops, bytes_accessed=size, transcendentals=0),
        **extra,
    )


def per_device(query_embed, truth_ids, text_embed, text_ids, texts, cores):
    rows, depth = query_embed.shape
    own = text_embed.shape[0]
    half = own // 2
    f32, bf16 = jnp.float32, jnp.bfloat16

    def permute(x, s):
        return lax.ppermute(x, "text", [(i, i ^ s) for i in range(texts)])

    packed = (depth // LANES) * rows + 16
    bundle = kernel(
        pack_queries, jax.ShapeDtypeStruct((1, packed, LANES), bf16), 4
    )(query_embed, truth_ids.reshape(1, rows))
    side = lax.rem(lax.axis_index("query"), 2)
    sent = kernel(
        pack_texts,
        jax.ShapeDtypeStruct((half + 16, depth), bf16),
        4,
        grid_spec=pltpu.PrefetchScalarGridSpec(
            num_scalar_prefetch=1,
            grid=(1,),
            in_specs=[
                pl.BlockSpec((half, depth), lambda i, c: (c[0], 0)),
                pl.BlockSpec((1, half), lambda i, c: (0, c[0])),
            ],
            out_specs=pl.BlockSpec((half + 16, depth), lambda i, c: (0, 0)),
        ),
    )(side.reshape(1), text_embed, text_ids.reshape(1, own))

    far_bits = []
    s = PAIR * 2
    while s < texts:
        far_bits.append(s)
        s *= 2
    for s in far_bits:
        bundle = jnp.concatenate([bundle, permute(bundle, s)], axis=0)
    near = permute(sent, PAIR)
    tiles = bundle.shape[0]
    bundles = [bundle] + [permute(bundle, d) for d in range(1, PLANE)]

    state_shape = jax.ShapeDtypeStruct((tiles, TOPK + 1, 8, LANES), f32)
    list_shape = jax.ShapeDtypeStruct((16, LANES), f32)
    flops = 2 * own * tiles * LANES * depth
    queries, wanted, state = kernel(
        lambda *refs: rank_own(*refs, tiles=tiles, rows=rows),
        [
            jax.ShapeDtypeStruct((tiles * LANES, depth), bf16),
            jax.ShapeDtypeStruct((tiles, 8, LANES), f32),
            state_shape,
        ],
        12,
        flops=flops,
        scratch_shapes=[pltpu.VMEM((own, tiles * LANES), f32), pltpu.VMEM((own, LANES), f32)],
    )(text_embed, text_ids.reshape(1, own), *bundles)
    far = lax.ppermute(near, "query", [(i, i ^ 1) for i in range(cores)])
    scratch = [pltpu.VMEM((half, tiles * LANES), f32), pltpu.VMEM((half, LANES), f32)]
    state = kernel(
        rank_near, state_shape, 8, flops=flops // 2, scratch_shapes=scratch
    )(near, queries, wanted, state)
    lists = kernel(
        rank_far, [list_shape] * tiles, 8, flops=flops // 2, scratch_shapes=scratch
    )(far, queries, wanted, state)
    lists = list(lists)
    for s in reversed(far_bits):
        mid = len(lists) // 2
        lists = [
            kernel(join, list_shape, 1)(lists[t], permute(lists[mid + t], s))
            for t in range(mid)
        ]
    mine = lists[0]
    top, margins = kernel(
        lambda *refs: finish(*refs, rows=rows),
        [jax.ShapeDtypeStruct((TOPK, rows), f32), jax.ShapeDtypeStruct((3, rows), f32)],
        1,
    )(mine, *[permute(mine, d) for d in range(1, PLANE)])
    return top.T, margins.T


def solution(mesh):
    texts, cores = mesh.shape["text"], mesh.shape["query"]
    return jax.shard_map(
        lambda *args: per_device(*args, texts=texts, cores=cores),
        mesh=mesh,
        in_specs=(P(("text", "query"), None), P(("text", "query")), P("text", None), P("text")),
        out_specs=(P(("text", "query"), None), P(("text", "query"), None)),
        check_vma=False,
    )
```

profile of v0, /device:TPU:0, one launch (start us, length us, event | category | flops | bytes accessed | tf_op | source)
XLA Modules:
  0.0 47.3 jit_solution(2435450287601851578)
XLA Ops:
  0.6 0.0 copy-start.3
  0.6 0.7 %copy-done.3 = s32[512]{0:T(512)S(1)} copy-done((s32[512]{0:T(512)S(1)}, s32[512]{0:T(512)}, u32[]{:S(2)}) %copy-start.3) | copy-done | bytes 2072
  1.3 0.0 copy-start
  1.3 1.2 %copy-done = bf16[512,1024]{1,0:T(8,128)(2,1)S(1)} copy-done((bf16[512,1024]{1,0:T(8,128)(2,1)S(1)}, bf16[512,1024]{1,0:T(8,128)(2,1)}, u32[]{:S(2)}) %copy-start) | copy-done | bytes 1048600
  2.5 0.0 copy-start.2
  2.5 0.0 copy-start.1
  2.6 0.0 copy-start.4
  2.6 3.1 %collective-permute-start = (bf16[272,1024]{1,0:T(8,128)(2,1)S(1)}, bf16[272,1024]{1,0:T(8,128)(2,1)S(1)}, u32[]{:S(2)}, u32[]{:S(2)}) collective-permute-start(bf16[272,1024]{1,0:T(8,128)(2,1)S(1)} %shard_map.59), channel_id=1, source_target_pairs={{0,8},{2,10},{4,12},{6,14},{8,0},{10,2},{12,4},{14,6},{16,24},{18,... | collective-permute-start | bytes 1671176 | tf_op jit(solution)/shard_map/ppermute | solution.py:215
  5.7 12.6 %collective-permute-done.near_ref = bf16[272,1024]{1,0:T(8,128)(2,1)S(1)} collective-permute-done((bf16[272,1024]{1,0:T(8,128)(2,1)S(1)}, bf16[272,1024]{1,0:T(8,128)(2,1)S(1)}, u32[]{:S(2)}, u32[]{:S(2)}) %collective-permute-start) | collective-permute-done | bytes 557088 | tf_op jit(solution)/shard_map/ppermute | solution.py:215
  18.3 0.0 collective-permute-start.1
  18.3 0.0 copy-done.2
  18.4 0.0 copy-done.4
  18.4 2.8 %collective-permute-start.2 = (bf16[1,272,128]{2,1,0:T(8,128)(2,1)S(1)}, bf16[1,272,128]{2,1,0:T(8,128)(2,1)S(1)}, u32[]{:S(2)}, u32[]{:S(2)}) collective-permute-start(bf16[1,272,128]{2,1,0:T(8,128)(2,1)S(1)} %shard_map.60), channel_id=1, source_target_pairs={{0,16},{2,18},{4,20},{6,22},{8,24},{10,26},{12,28},{14,30},{16,0},... | collective-permute-start | bytes 208904 | tf_op jit(solution)/shard_map/ppermute | solution.py:215
  21.2 4.3 %collective-permute-done.2 = bf16[1,272,128]{2,1,0:T(8,128)(2,1)S(1)} collective-permute-done((bf16[1,272,128]{2,1,0:T(8,128)(2,1)S(1)}, bf16[1,272,128]{2,1,0:T(8,128)(2,1)S(1)}, u32[]{:S(2)}, u32[]{:S(2)}) %collective-permute-start.2) | collective-permute-done | bytes 69664 | tf_op jit(solution)/shard_map/ppermute | solution.py:215
  25.6 2.6 %collective-permute-start.5 = (bf16[2,272,128]{2,1,0:T(8,128)(2,1)S(1)}, bf16[2,272,128]{2,1,0:T(8,128)(2,1)S(1)}, u32[]{:S(2)}, u32[]{:S(2)}) collective-permute-start(bf16[2,272,128]{2,1,0:T(8,128)(2,1)S(1)} %pad_maximum_fusion.refs_2_), channel_id=1, source_target_pairs={{0,6},{2,4},{4,2},{6,0},{8,14},{10,12},{12,10},{14,8},{16,22},{18,... | collective-permute-start | bytes 417800 | tf_op jit(solution)/shard_map/ppermute | solution.py:215
  28.1 0.5 %collective-permute-start.4 = (bf16[2,272,128]{2,1,0:T(8,128)(2,1)S(1)}, bf16[2,272,128]{2,1,0:T(8,128)(2,1)S(1)}, u32[]{:S(2)}, u32[]{:S(2)}) collective-permute-start(bf16[2,272,128]{2,1,0:T(8,128)(2,1)S(1)} %pad_maximum_fusion.refs_2_), channel_id=1, source_target_pairs={{0,4},{2,6},{4,0},{6,2},{8,12},{10,14},{12,8},{14,10},{16,20},{18,... | collective-permute-start | bytes 417800 | tf_op jit(solution)/shard_map/ppermute | solution.py:215
  28.6 0.5 %collective-permute-start.3 = (bf16[2,272,128]{2,1,0:T(8,128)(2,1)S(1)}, bf16[2,272,128]{2,1,0:T(8,128)(2,1)S(1)}, u32[]{:S(2)}, u32[]{:S(2)}) collective-permute-start(bf16[2,272,128]{2,1,0:T(8,128)(2,1)S(1)} %pad_maximum_fusion.refs_2_), channel_id=1, source_target_pairs={{0,2},{2,0},{4,6},{6,4},{8,10},{10,8},{12,14},{14,12},{16,18},{18,... | collective-permute-start | bytes 417800 | tf_op jit(solution)/shard_map/ppermute | solution.py:215
  29.1 3.8 %collective-permute-done.5.refs_5_ = bf16[2,272,128]{2,1,0:T(8,128)(2,1)S(1)} collective-permute-done((bf16[2,272,128]{2,1,0:T(8,128)(2,1)S(1)}, bf16[2,272,128]{2,1,0:T(8,128)(2,1)S(1)}, u32[]{:S(2)}, u32[]{:S(2)}) %collective-permute-start.5) | collective-permute-done | bytes 139296 | tf_op jit(solution)/shard_map/ppermute | solution.py:215
  32.9 1.0 %collective-permute-done.4.refs_4_ = bf16[2,272,128]{2,1,0:T(8,128)(2,1)S(1)} collective-permute-done((bf16[2,272,128]{2,1,0:T(8,128)(2,1)S(1)}, bf16[2,272,128]{2,1,0:T(8,128)(2,1)S(1)}, u32[]{:S(2)}, u32[]{:S(2)}) %collective-permute-start.4) | collective-permute-done | bytes 139296 | tf_op jit(solution)/shard_map/ppermute | solution.py:215
  33.9 0.0 collective-permute-done.3.refs_3_
  33.9 0.0 copy-done.1
  33.9 0.8 %shard_map.61 = (bf16[256,1024]{1,0:T(8,128)(2,1)S(1)}, f32[2,8,128]{2,1,0:T(8,128)S(1)}, f32[2,11,8,128]{3,2,1,0:T(8,128)S(1)}) custom-call(bf16[512,1024]{1,0:T(8,128)(2,1)S(1)} %copy-done.1, s32[1,512]{1,0:T(1,128)S(1)} %bitcast.6, bf16[2,272,128]{2,1,0:T(8,128)(2,1)S(1)} %pad_maximum_fusion.refs_2_, ...), custom_call_target="tpu_custom_call" | custom-call | flops 268435456 | bytes 622592 | tf_op jit(solution)/shard_map/pallas_call | solution.py:251
  34.7 0.5 %shard_map.62.state_ref = f32[2,11,8,128]{3,2,1,0:T(8,128)S(1)} custom-call(bf16[272,1024]{1,0:T(8,128)(2,1)S(1)} %collective-permute-done.near_ref, bf16[256,1024]{1,0:T(8,128)(2,1)S(1)} %get-tuple-element.9.query_ref, f32[2,8,128]{2,1,0:T(8,128)S(1)} %get-tuple-element.10.wanted_ref, f32[2,11,8,128]{3,2,1,0:T(8,128)S(1)} %get-tuple-element.11.state_ref), custom_call_target="tpu_custom_call" | custom-call | flops 134217728 | bytes 90112 | tf_op jit(solution)/shard_map/pallas_call | solution.py:264
  35.2 0.0 collective-permute-done.1.far_ref
  35.2 0.5 %shard_map.63 = (f32[16,128]{1,0:T(8,128)S(1)}, f32[16,128]{1,0:T(8,128)S(1)}) custom-call(bf16[272,1024]{1,0:T(8,128)(2,1)S(1)} %collective-permute-done.1.far_ref, bf16[256,1024]{1,0:T(8,128)(2,1)S(1)} %get-tuple-element.9.query_ref, f32[2,8,128]{2,1,0:T(8,128)S(1)} %get-tuple-element.10.wanted_ref, f32[2,11,8,128]{3,2,1,0:T(8,128)S(1)} %shard_map.62.state_ref), custom_call_target="tpu_custom_call" | custom-call | flops 134217728 | bytes 16384 | tf_op jit(solution)/shard_map/pallas_call | solution.py:267
  35.7 2.1 %collective-permute-start.6 = (f32[16,128]{1,0:T(8,128)S(1)}, f32[16,128]{1,0:T(8,128)S(1)}, u32[]{:S(2)}, u32[]{:S(2)}) collective-permute-start(f32[16,128]{1,0:T(8,128)S(1)} %get-tuple-element.13), channel_id=1, source_target_pairs={{0,16},{2,18},{4,20},{6,22},{8,24},{10,26},{12,28},{14,30},{16,0},... | collective-permute-start | bytes 24584 | tf_op jit(solution)/shard_map/ppermute | solution.py:215
  37.9 2.5 %collective-permute-done.6.theirs_ref = f32[16,128]{1,0:T(8,128)S(1)} collective-permute-done((f32[16,128]{1,0:T(8,128)S(1)}, f32[16,128]{1,0:T(8,128)S(1)}, u32[]{:S(2)}, u32[]{:S(2)}) %collective-permute-start.6) | collective-permute-done | bytes 8224 | tf_op jit(solution)/shard_map/ppermute | solution.py:215
  40.4 1.4 %collective-permute-start.9 = (f32[16,128]{1,0:T(8,128)S(1)}, f32[16,128]{1,0:T(8,128)S(1)}, u32[]{:S(2)}, u32[]{:S(2)}) collective-permute-start(f32[16,128]{1,0:T(8,128)S(1)} %shard_map.64.refs_0_), channel_id=1, source_target_pairs={{0,6},{2,4},{4,2},{6,0},{8,14},{10,12},{12,10},{14,8},{16,22},{18,... | collective-permute-start | bytes 24584 | tf_op jit(solution)/shard_map/ppermute | solution.py:215
  41.7 1.2 %collective-permute-start.8 = (f32[16,128]{1,0:T(8,128)S(1)}, f32[16,128]{1,0:T(8,128)S(1)}, u32[]{:S(2)}, u32[]{:S(2)}) collective-permute-start(f32[16,128]{1,0:T(8,128)S(1)} %shard_map.64.refs_0_), channel_id=1, source_target_pairs={{0,4},{2,6},{4,0},{6,2},{8,12},{10,14},{12,8},{14,10},{16,20},{18,... | collective-permute-start | bytes 24584 | tf_op jit(solution)/shard_map/ppermute | solution.py:215
  43.0 1.0 %collective-permute-start.7 = (f32[16,128]{1,0:T(8,128)S(1)}, f32[16,128]{1,0:T(8,128)S(1)}, u32[]{:S(2)}, u32[]{:S(2)}) collective-permute-start(f32[16,128]{1,0:T(8,128)S(1)} %shard_map.64.refs_0_), channel_id=1, source_target_pairs={{0,2},{2,0},{4,6},{6,4},{8,10},{10,8},{12,14},{14,12},{16,18},{18,... | collective-permute-start | bytes 24584 | tf_op jit(solution)/shard_map/ppermute | solution.py:215
  43.9 1.1 %collective-permute-done.9.refs_3_ = f32[16,128]{1,0:T(8,128)S(1)} collective-permute-done((f32[16,128]{1,0:T(8,128)S(1)}, f32[16,128]{1,0:T(8,128)S(1)}, u32[]{:S(2)}, u32[]{:S(2)}) %collective-permute-start.9) | collective-permute-done | bytes 8224 | tf_op jit(solution)/shard_map/ppermute | solution.py:215
  45.0 0.4 collective-permute-done.8.refs_2_
  45.4 1.2 %collective-permute-done.7.refs_1_ = f32[16,128]{1,0:T(8,128)S(1)} collective-permute-done((f32[16,128]{1,0:T(8,128)S(1)}, f32[16,128]{1,0:T(8,128)S(1)}, u32[]{:S(2)}, u32[]{:S(2)}) %collective-permute-start.7) | collective-permute-done | bytes 8224 | tf_op jit(solution)/shard_map/ppermute | solution.py:215
  46.6 0.7 %shard_map.65 = (f32[10,32]{1,0:T(8,128)}, f32[3,32]{1,0:T(4,128)}) custom-call(f32[16,128]{1,0:T(8,128)S(1)} %shard_map.64.refs_0_, f32[16,128]{1,0:T(8,128)S(1)} %collective-permute-done.7.refs_1_, f32[16,128]{1,0:T(8,128)S(1)} %collective-permute-done.8.refs_2_, f32[16,128]{1,0:T(8,128)S(1)} %collective-permute-done.9.refs_3_), custom_call_target="tpu_custom_call" | custom-call | bytes 1664 | tf_op jit(solution)/shard_map/pallas_call | solution.py:278
  (4 shorter events, 0.1 us)
Async XLA Ops:
  0.6 0.7 %copy-start.3 = (s32[512]{0:T(512)S(1)}, s32[512]{0:T(512)}, u32[]{:S(2)}) copy-start(s32[512]{0:T(512)} %param.7) | copy-start | bytes 6148
  1.3 1.2 %copy-start = (bf16[512,1024]{1,0:T(8,128)(2,1)S(1)}, bf16[512,1024]{1,0:T(8,128)(2,1)}, u32[]{:S(2)}) copy-start(bf16[512,1024]{1,0:T(8,128)(2,1)} %refs_0_.1) | copy-start | bytes 3145732
  2.5 15.8 %copy-start.2 = (bf16[32,1024]{1,0:T(8,128)(2,1)S(1)}, bf16[32,1024]{1,0:T(8,128)(2,1)}, u32[]{:S(2)}) copy-start(bf16[32,1024]{1,0:T(8,128)(2,1)} %query_ref.1) | copy-start | bytes 196612
  2.5 31.3 %copy-start.1 = (bf16[512,1024]{1,0:T(8,128)(2,1)S(1)}, bf16[512,1024]{1,0:T(8,128)(2,1)}, u32[]{:S(2)}) copy-start(bf16[512,1024]{1,0:T(8,128)(2,1)} %refs_0_.1) | copy-start | bytes 3145732
  2.6 15.8 %copy-start.4 = (s32[32]{0:T(128)S(1)}, s32[32]{0:T(128)}, u32[]{:S(2)}) copy-start(s32[32]{0:T(128)} %param.5) | copy-start | bytes 388
  2.6 15.7 %collective-permute-start = (bf16[272,1024]{1,0:T(8,128)(2,1)S(1)}, bf16[272,1024]{1,0:T(8,128)(2,1)S(1)}, u32[]{:S(2)}, u32[]{:S(2)}) collective-permute-start(bf16[272,1024]{1,0:T(8,128)(2,1)S(1)} %shard_map.59), channel_id=1, source_target_pairs={{0,8},{2,10},{4,12},{6,14},{8,0},{10,2},{12,4},{14,6},{16,24},{18,... | collective-permute-start | bytes 1671176 | tf_op jit(solution)/shard_map/ppermute | solution.py:215
  18.3 16.8 %collective-permute-start.1 = (bf16[272,1024]{1,0:T(8,128)(2,1)S(1)}, bf16[272,1024]{1,0:T(8,128)(2,1)S(1)}, u32[]{:S(2)}, u32[]{:S(2)}) collective-permute-start(bf16[272,1024]{1,0:T(8,128)(2,1)S(1)} %collective-permute-done.near_ref), channel_id=1, source_target_pairs={{0,1},{1,0},{2,3},{3,2},{4,5},{5,4},{6,7},{7,6},{8,9},{9,8},{10,11... | collective-permute-start | bytes 1671176 | tf_op jit(solution)/shard_map/ppermute | solution.py:262
  18.4 7.2 %collective-permute-start.2 = (bf16[1,272,128]{2,1,0:T(8,128)(2,1)S(1)}, bf16[1,272,128]{2,1,0:T(8,128)(2,1)S(1)}, u32[]{:S(2)}, u32[]{:S(2)}) collective-permute-start(bf16[1,272,128]{2,1,0:T(8,128)(2,1)S(1)} %shard_map.60), channel_id=1, source_target_pairs={{0,16},{2,18},{4,20},{6,22},{8,24},{10,26},{12,28},{14,30},{16,0},... | collective-permute-start | bytes 208904 | tf_op jit(solution)/shard_map/ppermute | solution.py:215
  25.6 7.3 %collective-permute-start.5 = (bf16[2,272,128]{2,1,0:T(8,128)(2,1)S(1)}, bf16[2,272,128]{2,1,0:T(8,128)(2,1)S(1)}, u32[]{:S(2)}, u32[]{:S(2)}) collective-permute-start(bf16[2,272,128]{2,1,0:T(8,128)(2,1)S(1)} %pad_maximum_fusion.refs_2_), channel_id=1, source_target_pairs={{0,6},{2,4},{4,2},{6,0},{8,14},{10,12},{12,10},{14,8},{16,22},{18,... | collective-permute-start | bytes 417800 | tf_op jit(solution)/shard_map/ppermute | solution.py:215
  28.1 5.7 %collective-permute-start.4 = (bf16[2,272,128]{2,1,0:T(8,128)(2,1)S(1)}, bf16[2,272,128]{2,1,0:T(8,128)(2,1)S(1)}, u32[]{:S(2)}, u32[]{:S(2)}) collective-permute-start(bf16[2,272,128]{2,1,0:T(8,128)(2,1)S(1)} %pad_maximum_fusion.refs_2_), channel_id=1, source_target_pairs={{0,4},{2,6},{4,0},{6,2},{8,12},{10,14},{12,8},{14,10},{16,20},{18,... | collective-permute-start | bytes 417800 | tf_op jit(solution)/shard_map/ppermute | solution.py:215
  28.6 5.2 %collective-permute-start.3 = (bf16[2,272,128]{2,1,0:T(8,128)(2,1)S(1)}, bf16[2,272,128]{2,1,0:T(8,128)(2,1)S(1)}, u32[]{:S(2)}, u32[]{:S(2)}) collective-permute-start(bf16[2,272,128]{2,1,0:T(8,128)(2,1)S(1)} %pad_maximum_fusion.refs_2_), channel_id=1, source_target_pairs={{0,2},{2,0},{4,6},{6,4},{8,10},{10,8},{12,14},{14,12},{16,18},{18,... | collective-permute-start | bytes 417800 | tf_op jit(solution)/shard_map/ppermute | solution.py:215
  35.7 4.6 %collective-permute-start.6 = (f32[16,128]{1,0:T(8,128)S(1)}, f32[16,128]{1,0:T(8,128)S(1)}, u32[]{:S(2)}, u32[]{:S(2)}) collective-permute-start(f32[16,128]{1,0:T(8,128)S(1)} %get-tuple-element.13), channel_id=1, source_target_pairs={{0,16},{2,18},{4,20},{6,22},{8,24},{10,26},{12,28},{14,30},{16,0},... | collective-permute-start | bytes 24584 | tf_op jit(solution)/shard_map/ppermute | solution.py:215
  40.4 4.6 %collective-permute-start.9 = (f32[16,128]{1,0:T(8,128)S(1)}, f32[16,128]{1,0:T(8,128)S(1)}, u32[]{:S(2)}, u32[]{:S(2)}) collective-permute-start(f32[16,128]{1,0:T(8,128)S(1)} %shard_map.64.refs_0_), channel_id=1, source_target_pairs={{0,6},{2,4},{4,2},{6,0},{8,14},{10,12},{12,10},{14,8},{16,22},{18,... | collective-permute-start | bytes 24584 | tf_op jit(solution)/shard_map/ppermute | solution.py:215
  41.7 3.7 %collective-permute-start.8 = (f32[16,128]{1,0:T(8,128)S(1)}, f32[16,128]{1,0:T(8,128)S(1)}, u32[]{:S(2)}, u32[]{:S(2)}) collective-permute-start(f32[16,128]{1,0:T(8,128)S(1)} %shard_map.64.refs_0_), channel_id=1, source_target_pairs={{0,4},{2,6},{4,0},{6,2},{8,12},{10,14},{12,8},{14,10},{16,20},{18,... | collective-permute-start | bytes 24584 | tf_op jit(solution)/shard_map/ppermute | solution.py:215
  43.0 3.7 %collective-permute-start.7 = (f32[16,128]{1,0:T(8,128)S(1)}, f32[16,128]{1,0:T(8,128)S(1)}, u32[]{:S(2)}, u32[]{:S(2)}) collective-permute-start(f32[16,128]{1,0:T(8,128)S(1)} %shard_map.64.refs_0_), channel_id=1, source_target_pairs={{0,2},{2,0},{4,6},{6,4},{8,10},{10,8},{12,14},{14,12},{16,18},{18,... | collective-permute-start | bytes 24584 | tf_op jit(solution)/shard_map/ppermute | solution.py:215
where the time goes:
time: 47.8 us; the launch traced here: 47.3 us
  waiting for transfers between devices  26.9 us (56%)
  starting transfers between devices  15.2 us (32%)
  Pallas kernels  2.6 us (5%)
  local copies, waits for them, and re-layouts  1.91 us (4%)
  between operations  0.71 us (1%)
    ppermute x9, waiting for transfers between devices, permute(): return lax.ppermute(x, 'text', [(i, i ^ s) for i in range(texts)])  26.9 us
    ppermute x9, starting transfers between devices, permute(): return lax.ppermute(x, 'text', [(i, i ^ s) for i in range(texts)])  15.2 us
    unnamed x10, local copies, waits for them, and re-layouts  1.91 us
  transfers between devices with their start and end apart: 10, of which 8 were waited for; matrix products, arithmetic and copies ran while one was open for 0% of the time, Pallas kernels for 3%

commit v1 on v0

--- a/solution.py
+++ b/solution.py
@@ -8,6 +8,7 @@
 TOPK = 10
 LANES = 128
 PLANE = 4
+PARTS = 2
 PAIR = 4
 
 
@@ -50,29 +51,31 @@
     return head + tail
 
 
-def pack_queries(query_ref, ids_ref, out_ref):
+def digits_of(ids):
+    high = (ids >> 8).astype(jnp.float32)
+    low = (ids & 255).astype(jnp.float32)
+    row = lax.broadcasted_iota(jnp.int32, (16, ids.shape[1]), 0)
+    return jnp.where(row == 0, high, jnp.where(row == 1, low, 0.0)).astype(jnp.bfloat16)
+
+
+def pack_queries(query_ref, wanted_ref, block_ref):
     rows, depth = query_ref.shape
     columns = depth // LANES
     for j in range(columns):
-        out_ref[0, j * rows : (j + 1) * rows, :] = query_ref[:, j * LANES : (j + 1) * LANES]
-    ids = jnp.concatenate([ids_ref[...], jnp.zeros((1, LANES - rows), jnp.int32)], axis=1)
-    high = (ids >> 8).astype(jnp.float32)
-    low = (ids & 255).astype(jnp.float32)
-    row = lax.broadcasted_iota(jnp.int32, (16, LANES), 0)
-    digits = jnp.where(row == 0, high, jnp.where(row == 1, low, 0.0))
-    out_ref[0, columns * rows :, :] = digits.astype(jnp.bfloat16)
-
-
-def pack_texts(core_ref, text_ref, ids_ref, out_ref):
-    half, depth = text_ref.shape
-    out_ref[:half, :] = text_ref[...]
-    row = lax.broadcasted_iota(jnp.int32, (16, half), 0)
-    ids = ids_ref[...]
-    high = (ids >> 8).astype(jnp.float32)
-    low = (ids & 255).astype(jnp.float32)
-    digits = jnp.where(row == 0, high, jnp.where(row == 1, low, 0.0))
-    out_ref[half:, :half] = digits.astype(jnp.bfloat16)
-    out_ref[half:, half:] = jnp.zeros((16, depth - half), jnp.bfloat16)
+        block_ref[0, j * rows : (j + 1) * rows, :] = query_ref[:, j * LANES : (j + 1) * LANES]
+    ids = jnp.concatenate([wanted_ref[...], jnp.zeros((1, LANES - rows), jnp.int32)], axis=1)
+    block_ref[0, columns * rows :, :] = digits_of(ids)
+
+
+def pack_texts(text_ref, ids_ref, *part_refs):
+    part, depth = part_refs[-1].shape[0] - (8 if len(part_refs) == 1 else 0), text_ref.shape[1]
+    half = part * len(part_refs)
+    start = pl.multiple_of(lax.rem(lax.axis_index("query"), 2) * half, half)
+    for n, part_ref in enumerate(part_refs):
+        part_ref[:part, :] = text_ref[pl.ds(pl.multiple_of(start + n * part, part), part), :]
+    first_ref = part_refs[0]
+    first_ref[part:, :half] = digits_of(ids_ref[:, pl.ds(start, half)])[:8]
+    first_ref[part:, half:] = jnp.zeros((8, depth - half), jnp.bfloat16)
 
 
 def scan(text_ref, queries, label_ref, score_ref, wanted, states):
@@ -113,8 +116,14 @@
     return digits[0:1] * 256.0 + digits[1:2]
 
 
+def blank(state_ref):
+    for i in range(TOPK + 1):
+        state_ref[i] = jnp.full((8, LANES), -jnp.inf if i < TOPK else 0.0, jnp.float32)
+
+
 def rank_own(*refs, tiles, rows):
-    text_ref, ids_ref = refs[:2]
+    text_ref, ids_ref, blank_ref = refs[:3]
+    refs = refs[1:]
     bundles = refs[2 : 2 + PLANE]
     query_ref, wanted_ref, state_ref, score_ref, label_ref = refs[2 + PLANE :]
     columns = text_ref.shape[1] // LANES
@@ -124,40 +133,54 @@
         total = jnp.zeros((1, LANES), jnp.float32)
         for d in range(PLANE):
             at = slice(h * LANES + d * rows, h * LANES + (d + 1) * rows)
+            source = bundles[d].at[h]
             for j in range(columns):
-                block = bundles[d][h, j * rows : (j + 1) * rows, :]
-                query_ref[at, j * LANES : (j + 1) * LANES] = block
-            here = joined(bundles[d][h, columns * rows :, :])
+                query_ref[at, j * LANES : (j + 1) * LANES] = source[j * rows : (j + 1) * rows, :]
+            here = joined(source[columns * rows :, :])
             total = total + (here if d == 0 else pltpu.roll(here, d * rows, 1))
         wanted.append(jnp.broadcast_to(total, (8, LANES)))
         wanted_ref[h] = wanted[h]
-    low = jnp.full((8, LANES), -jnp.inf, jnp.float32)
-    start = [low] * TOPK + [jnp.zeros((8, LANES), jnp.float32)]
+    start = [blank_ref[i] for i in range(TOPK + 1)]
     states = scan(text_ref, query_ref[...], label_ref, score_ref, wanted, [start] * tiles)
     for h in range(tiles):
         for i in range(TOPK + 1):
             state_ref[h, i] = states[h][i]
 
 
-def scan_more(part_ref, query_ref, wanted_ref, state_ref, score_ref, label_ref):
-    half = part_ref.shape[0] - 16
+def load_states(wanted_ref, state_ref):
     tiles = state_ref.shape[0]
-    spread(joined(part_ref[half:, :half]), label_ref)
     wanted = [wanted_ref[h] for h in range(tiles)]
-    states = [[state_ref[h, i] for i in range(TOPK + 1)] for h in range(tiles)]
+    return wanted, [[state_ref[h, i] for i in range(TOPK + 1)] for h in range(tiles)]
+
+
+def scan_part(part_ref, first_ref, count, query_ref, wanted, states, score_ref, label_ref, part):
+    at = slice(part * count, (part + 1) * count)
+    spread(joined(first_ref[count:, at]), label_ref)
     return scan(part_ref, query_ref[...], label_ref, score_ref, wanted, states)
 
 
-def rank_near(near_ref, query_ref, wanted_ref, state_ref, next_ref, score_ref, label_ref):
-    states = scan_more(near_ref, query_ref, wanted_ref, state_ref, score_ref, label_ref)
+def rank_parts(*refs, parts):
+    part_refs, refs = refs[: len(parts)], refs[len(parts) :]
+    first_refs, refs = refs[: len(parts)], refs[len(parts) :]
+    query_ref, wanted_ref, state_ref, next_ref, score_ref, label_ref = refs
+    count = score_ref.shape[0]
+    wanted, states = load_states(wanted_ref, state_ref)
+    for part_ref, first_ref, part in zip(part_refs, first_refs, parts):
+        states = scan_part(
+            part_ref, first_ref, count, query_ref, wanted, states, score_ref, label_ref, part
+        )
     for h, state in enumerate(states):
         for i in range(TOPK + 1):
             next_ref[h, i] = state[i]
 
 
-def rank_far(far_ref, query_ref, wanted_ref, state_ref, *refs):
+def rank_last(part_ref, first_ref, query_ref, wanted_ref, state_ref, *refs, part):
     outs, (score_ref, label_ref) = refs[:-2], refs[-2:]
-    states = scan_more(far_ref, query_ref, wanted_ref, state_ref, score_ref, label_ref)
+    count = score_ref.shape[0]
+    wanted, states = load_states(wanted_ref, state_ref)
+    states = scan_part(
+        part_ref, first_ref, count, query_ref, wanted, states, score_ref, label_ref, part
+    )
     for out_ref, state in zip(outs, states):
         best, truth = list(state[:TOPK]), state[TOPK]
         for shift in (4, 2, 1):
@@ -208,40 +231,28 @@
 def per_device(query_embed, truth_ids, text_embed, text_ids, texts, cores):
     rows, depth = query_embed.shape
     own = text_embed.shape[0]
-    half = own // 2
     f32, bf16 = jnp.float32, jnp.bfloat16
 
     def permute(x, s):
         return lax.ppermute(x, "text", [(i, i ^ s) for i in range(texts)])
 
     packed = (depth // LANES) * rows + 16
-    bundle = kernel(
-        pack_queries, jax.ShapeDtypeStruct((1, packed, LANES), bf16), 4
-    )(query_embed, truth_ids.reshape(1, rows))
-    side = lax.rem(lax.axis_index("query"), 2)
+    pack = kernel(pack_queries, jax.ShapeDtypeStruct((1, packed, LANES), bf16), 1)
+    empty = kernel(blank, jax.ShapeDtypeStruct((TOPK + 1, 8, LANES), f32), 1, flops=4 * 10**9)()
+    bundle = pack(query_embed, truth_ids.reshape(1, rows))
+    part = own // 2 // PARTS
     sent = kernel(
         pack_texts,
-        jax.ShapeDtypeStruct((half + 16, depth), bf16),
-        4,
-        grid_spec=pltpu.PrefetchScalarGridSpec(
-            num_scalar_prefetch=1,
-            grid=(1,),
-            in_specs=[
-                pl.BlockSpec((half, depth), lambda i, c: (c[0], 0)),
-                pl.BlockSpec((1, half), lambda i, c: (0, c[0])),
-            ],
-            out_specs=pl.BlockSpec((half + 16, depth), lambda i, c: (0, 0)),
-        ),
-    )(side.reshape(1), text_embed, text_ids.reshape(1, own))
-
+        [jax.ShapeDtypeStruct((part + (8 if n == 0 else 0), depth), bf16) for n in range(PARTS)],
+        1,
+    )(text_embed, text_ids.reshape(1, own))
+    near = [permute(x, PAIR) for x in sent]
     far_bits = []
-    s = PAIR * 2
+    s = 2 * PAIR
     while s < texts:
+        bundle = jnp.concatenate([bundle, permute(bundle, s)], axis=0)
         far_bits.append(s)
         s *= 2
-    for s in far_bits:
-        bundle = jnp.concatenate([bundle, permute(bundle, s)], axis=0)
-    near = permute(sent, PAIR)
     tiles = bundle.shape[0]
     bundles = [bundle] + [permute(bundle, d) for d in range(1, PLANE)]
 
@@ -258,15 +269,39 @@
         12,
         flops=flops,
         scratch_shapes=[pltpu.VMEM((own, tiles * LANES), f32), pltpu.VMEM((own, LANES), f32)],
-    )(text_embed, text_ids.reshape(1, own), *bundles)
-    far = lax.ppermute(near, "query", [(i, i ^ 1) for i in range(cores)])
-    scratch = [pltpu.VMEM((half, tiles * LANES), f32), pltpu.VMEM((half, LANES), f32)]
-    state = kernel(
-        rank_near, state_shape, 8, flops=flops // 2, scratch_shapes=scratch
-    )(near, queries, wanted, state)
+    )(text_embed, text_ids.reshape(1, own), empty, *bundles)
+    far = []
+    for x in near:
+        far.append(lax.ppermute(x, "query", [(i, i ^ 1) for i in range(cores)]))
+    scratch = [pltpu.VMEM((part, tiles * LANES), f32), pltpu.VMEM((part, LANES), f32)]
+    flops = flops // 2 // PARTS
+
+    def rank(parts):
+        return kernel(
+            lambda *refs: rank_parts(*refs, parts=[n for n, m in parts]),
+            state_shape,
+            8,
+            flops=flops * len(parts),
+            scratch_shapes=scratch,
+        )(
+            *[(far if m else near)[n] for n, m in parts],
+            *[(far if m else near)[0] for n, m in parts],
+            queries,
+            wanted,
+            state,
+        )
+
+    last = PARTS - 1
+    if last:
+        state = rank([(n, m) for n in range(last) for m in (0, 1)])
+    state = rank([(last, 0)])
     lists = kernel(
-        rank_far, [list_shape] * tiles, 8, flops=flops // 2, scratch_shapes=scratch
-    )(far, queries, wanted, state)
+        lambda *refs: rank_last(*refs, part=last),
+        [list_shape] * tiles,
+        8,
+        flops=flops,
+        scratch_shapes=scratch,
+    )(far[last], far[0], queries, wanted, state)
     lists = list(lists)
     for s in reversed(far_bits):
         mid = len(lists) // 2

time: 47.8 us -> 42 us (0.88)
  waiting for transfers between devices: 26.9 us -> 18.9 us
  starting transfers between devices: 15.2 us -> 16.8 us
  local copies, waits for them, and re-layouts: 1.91 us -> 2.48 us
    ppermute x9 -> x10, waiting for transfers between devices: 26.9 us -> 18.9 us  [permute(): return lax.ppermute(x, 'text', [(i, i ^ s) for i in range(texts)])]
    ppermute x9 -> x10, starting transfers between devices: 15.2 us -> 16.3 us  [permute(): return lax.ppermute(x, 'text', [(i, i ^ s) for i in range(texts)])]
    unnamed x10 -> x12, local copies, waits for them, and re-layouts: 1.91 us -> 2.48 us
    ppermute x1 -> x2, starting transfers between devices: 0.01 us -> 0.51 us  [per_device(): far.append(lax.ppermute(x, 'query', [(i, i ^ 1) for i in range(cores)]))]
    pallas_call x4 -> x6, Pallas kernels: 1.09 us -> 1.35 us  [the longest x2 0.9 us: rank(): kernel(lambda *refs: rank_parts(*refs, parts=[n for n, m in parts]), stat...]
  transfers between devices with their start and end apart: 10 -> 12, of which waited for: 8 -> 6; matrix products, arithmetic and copies ran while one was open for 0% -> 0% of each run, Pallas kernels for 3% -> 4%
where the time goes in v1:
time: 42 us; the launch traced here: 41.7 us
  waiting for transfers between devices  18.9 us (45%)
  starting transfers between devices  16.8 us (40%)
  Pallas kernels  2.85 us (7%)
  local copies, waits for them, and re-layouts  2.48 us (6%)
  between operations  0.73 us (2%)
    ppermute x10, waiting for transfers between devices, permute(): return lax.ppermute(x, 'text', [(i, i ^ s) for i in range(texts)])  18.9 us
    ppermute x10, starting transfers between devices, permute(): return lax.ppermute(x, 'text', [(i, i ^ s) for i in range(texts)])  16.3 us
    unnamed x12, local copies, waits for them, and re-layouts  2.48 us
    pallas_call x2, Pallas kernels, rank(): kernel(lambda *refs: rank_parts(*refs, parts=[n for n, m in parts]), stat...  0.9 us
  transfers between devices with their start and end apart: 12, of which 6 were waited for; matrix products, arithmetic and copies ran while one was open for 0% of the time, Pallas kernels for 4%

profile of v1, /device:TPU:0, one launch (start us, length us, event | category | flops | bytes accessed | tf_op | source)
XLA Modules:
  0.0 41.7 jit_solution(16690295681447267218)
XLA Ops:
  0.6 0.0 copy-start
  0.6 1.2 %copy-done = bf16[512,1024]{1,0:T(8,128)(2,1)S(1)} copy-done((bf16[512,1024]{1,0:T(8,128)(2,1)S(1)}, bf16[512,1024]{1,0:T(8,128)(2,1)}, u32[]{:S(2)}) %copy-start) | copy-done | bytes 1048600
  1.9 0.0 copy-start.3
  1.9 0.7 %copy-done.3 = s32[512]{0:T(512)S(1)} copy-done((s32[512]{0:T(512)S(1)}, s32[512]{0:T(512)}, u32[]{:S(2)}) %copy-start.3) | copy-done | bytes 2072
  2.5 0.0 copy-start.2
  2.6 3.1 %collective-permute-start.2 = (bf16[136,1024]{1,0:T(8,128)(2,1)S(1)}, bf16[136,1024]{1,0:T(8,128)(2,1)S(1)}, u32[]{:S(2)}, u32[]{:S(2)}) collective-permute-start(bf16[136,1024]{1,0:T(8,128)(2,1)S(1)} %get-tuple-element.12), channel_id=1, source_target_pairs={{0,8},{2,10},{4,12},{6,14},{8,0},{10,2},{12,4},{14,6},{16,24},{18,... | collective-permute-start | bytes 835592 | tf_op jit(solution)/shard_map/ppermute | solution.py:237
  5.7 0.0 copy-start.5
  5.7 0.1 collective-permute-start
  5.8 0.0 copy-done.2
  5.8 0.6 %copy-done.5 = s32[32]{0:T(128)S(1)} copy-done((s32[32]{0:T(128)S(1)}, s32[32]{0:T(128)}, u32[]{:S(2)}) %copy-start.5) | copy-done | bytes 152
  6.4 2.7 %collective-permute-start.4 = (bf16[1,272,128]{2,1,0:T(8,128)(2,1)S(1)}, bf16[1,272,128]{2,1,0:T(8,128)(2,1)S(1)}, u32[]{:S(2)}, u32[]{:S(2)}) collective-permute-start(bf16[1,272,128]{2,1,0:T(8,128)(2,1)S(1)} %shard_map.61), channel_id=1, source_target_pairs={{0,16},{2,18},{4,20},{6,22},{8,24},{10,26},{12,28},{14,30},{16,0},... | collective-permute-start | bytes 208904 | tf_op jit(solution)/shard_map/ppermute | solution.py:237
  9.0 9.7 %collective-permute-done.4 = bf16[1,272,128]{2,1,0:T(8,128)(2,1)S(1)} collective-permute-done((bf16[1,272,128]{2,1,0:T(8,128)(2,1)S(1)}, bf16[1,272,128]{2,1,0:T(8,128)(2,1)S(1)}, u32[]{:S(2)}, u32[]{:S(2)}) %collective-permute-start.4) | collective-permute-done | bytes 69664 | tf_op jit(solution)/shard_map/ppermute | solution.py:237
  18.7 0.0 copy-start.1
  18.8 0.0 copy-start.4
  18.8 1.6 %collective-permute-start.5 = (bf16[2,272,128]{2,1,0:T(8,128)(2,1)S(1)}, bf16[2,272,128]{2,1,0:T(8,128)(2,1)S(1)}, u32[]{:S(2)}, u32[]{:S(2)}) collective-permute-start(bf16[2,272,128]{2,1,0:T(8,128)(2,1)S(1)} %pad_maximum_fusion.refs_3_), channel_id=1, source_target_pairs={{0,2},{2,0},{4,6},{6,4},{8,10},{10,8},{12,14},{14,12},{16,18},{18,... | collective-permute-start | bytes 417800 | tf_op jit(solution)/shard_map/ppermute | solution.py:237
  20.3 1.5 %collective-permute-start.6 = (bf16[2,272,128]{2,1,0:T(8,128)(2,1)S(1)}, bf16[2,272,128]{2,1,0:T(8,128)(2,1)S(1)}, u32[]{:S(2)}, u32[]{:S(2)}) collective-permute-start(bf16[2,272,128]{2,1,0:T(8,128)(2,1)S(1)} %pad_maximum_fusion.refs_3_), channel_id=1, source_target_pairs={{0,4},{2,6},{4,0},{6,2},{8,12},{10,14},{12,8},{14,10},{16,20},{18,... | collective-permute-start | bytes 417800 | tf_op jit(solution)/shard_map/ppermute | solution.py:237
  21.8 0.5 %collective-permute-start.7 = (bf16[2,272,128]{2,1,0:T(8,128)(2,1)S(1)}, bf16[2,272,128]{2,1,0:T(8,128)(2,1)S(1)}, u32[]{:S(2)}, u32[]{:S(2)}) collective-permute-start(bf16[2,272,128]{2,1,0:T(8,128)(2,1)S(1)} %pad_maximum_fusion.refs_3_), channel_id=1, source_target_pairs={{0,6},{2,4},{4,2},{6,0},{8,14},{10,12},{12,10},{14,8},{16,22},{18,... | collective-permute-start | bytes 417800 | tf_op jit(solution)/shard_map/ppermute | solution.py:237
  22.3 0.0 collective-permute-done.refs_0_
  22.3 0.0 collective-permute-start.1
  22.3 0.0 collective-permute-done.2.refs_0_.refs_2_.refs_1_
  22.3 0.5 %collective-permute-start.3 = (bf16[136,1024]{1,0:T(8,128)(2,1)S(1)}, bf16[136,1024]{1,0:T(8,128)(2,1)S(1)}, u32[]{:S(2)}, u32[]{:S(2)}) collective-permute-start(bf16[136,1024]{1,0:T(8,128)(2,1)S(1)} %collective-permute-done.2.refs_0_.refs_2_.refs_1_), channel_id=1, source_target_pairs={{0,1},{1,0},{2,3},{3,2},{4,5},{5,4},{6,7},{7,6},{8,9},{9,8},{10,11... | collective-permute-start | bytes 835592 | tf_op jit(solution)/shard_map/ppermute | solution.py:275
  22.8 2.1 %collective-permute-done.5.refs_4_ = bf16[2,272,128]{2,1,0:T(8,128)(2,1)S(1)} collective-permute-done((bf16[2,272,128]{2,1,0:T(8,128)(2,1)S(1)}, bf16[2,272,128]{2,1,0:T(8,128)(2,1)S(1)}, u32[]{:S(2)}, u32[]{:S(2)}) %collective-permute-start.5) | collective-permute-done | bytes 139296 | tf_op jit(solution)/shard_map/ppermute | solution.py:237
  25.0 3.3 %collective-permute-done.6.refs_5_ = bf16[2,272,128]{2,1,0:T(8,128)(2,1)S(1)} collective-permute-done((bf16[2,272,128]{2,1,0:T(8,128)(2,1)S(1)}, bf16[2,272,128]{2,1,0:T(8,128)(2,1)S(1)}, u32[]{:S(2)}, u32[]{:S(2)}) %collective-permute-start.6) | collective-permute-done | bytes 139296 | tf_op jit(solution)/shard_map/ppermute | solution.py:237
  28.3 0.0 collective-permute-done.7.refs_6_
  28.3 0.0 copy-done.1
  28.3 0.0 copy-done.4
  28.3 0.8 %shard_map.62 = (bf16[256,1024]{1,0:T(8,128)(2,1)S(1)}, f32[2,8,128]{2,1,0:T(8,128)S(1)}, f32[2,11,8,128]{3,2,1,0:T(8,128)S(1)}) custom-call(bf16[512,1024]{1,0:T(8,128)(2,1)S(1)} %copy-done.1, s32[1,512]{1,0:T(1,128)S(1)} %bitcast.5, f32[11,8,128]{2,1,0:T(8,128)S(1)} %shard_map.60.refs_2_, bf16[2,272,128]{2,1,0:T(8,128)(2,1)S(1)} %pad_maximum_fusion.refs_3_, ...), custom_call_target="tpu_custom_call" | custom-call | flops 268435456 | bytes 622592 | tf_op jit(solution)/shard_map/pallas_call | solution.py:262
  29.1 0.0 collective-permute-done.3.refs_1_.refs_3_
  29.1 0.6 %shard_map.63.refs_4_ = f32[2,11,8,128]{3,2,1,0:T(8,128)S(1)} custom-call(bf16[136,1024]{1,0:T(8,128)(2,1)S(1)} %collective-permute-done.2.refs_0_.refs_2_.refs_1_, bf16[136,1024]{1,0:T(8,128)(2,1)S(1)} %collective-permute-done.3.refs_1_.refs_3_, bf16[136,1024]{1,0:T(8,128)(2,1)S(1)} %collective-permute-done.2.refs_0_.refs_2_.refs_1_, ...), custom_call_target="tpu_custom_call" | custom-call | flops 134217728 | bytes 90112 | tf_op jit(solution)/shard_map/pallas_call | solution.py:280
  29.7 0.3 shard_map.64.refs_4_
  30.0 0.0 collective-permute-done.1.refs_0_
  30.0 0.4 shard_map.65
  30.4 3.3 %collective-permute-start.8 = (f32[16,128]{1,0:T(8,128)S(1)}, f32[16,128]{1,0:T(8,128)S(1)}, u32[]{:S(2)}, u32[]{:S(2)}) collective-permute-start(f32[16,128]{1,0:T(8,128)S(1)} %get-tuple-element.17), channel_id=1, source_target_pairs={{0,16},{2,18},{4,20},{6,22},{8,24},{10,26},{12,28},{14,30},{16,0},... | collective-permute-start | bytes 24584 | tf_op jit(solution)/shard_map/ppermute | solution.py:237
  33.7 1.6 %collective-permute-done.8.theirs_ref = f32[16,128]{1,0:T(8,128)S(1)} collective-permute-done((f32[16,128]{1,0:T(8,128)S(1)}, f32[16,128]{1,0:T(8,128)S(1)}, u32[]{:S(2)}, u32[]{:S(2)}) %collective-permute-start.8) | collective-permute-done | bytes 8224 | tf_op jit(solution)/shard_map/ppermute | solution.py:237
  35.4 1.1 %collective-permute-start.10 = (f32[16,128]{1,0:T(8,128)S(1)}, f32[16,128]{1,0:T(8,128)S(1)}, u32[]{:S(2)}, u32[]{:S(2)}) collective-permute-start(f32[16,128]{1,0:T(8,128)S(1)} %shard_map.66.refs_0_), channel_id=1, source_target_pairs={{0,4},{2,6},{4,0},{6,2},{8,12},{10,14},{12,8},{14,10},{16,20},{18,... | collective-permute-start | bytes 24584 | tf_op jit(solution)/shard_map/ppermute | solution.py:237
  36.5 0.8 %collective-permute-start.11 = (f32[16,128]{1,0:T(8,128)S(1)}, f32[16,128]{1,0:T(8,128)S(1)}, u32[]{:S(2)}, u32[]{:S(2)}) collective-permute-start(f32[16,128]{1,0:T(8,128)S(1)} %shard_map.66.refs_0_), channel_id=1, source_target_pairs={{0,6},{2,4},{4,2},{6,0},{8,14},{10,12},{12,10},{14,8},{16,22},{18,... | collective-permute-start | bytes 24584 | tf_op jit(solution)/shard_map/ppermute | solution.py:237
  37.3 1.7 %collective-permute-start.9 = (f32[16,128]{1,0:T(8,128)S(1)}, f32[16,128]{1,0:T(8,128)S(1)}, u32[]{:S(2)}, u32[]{:S(2)}) collective-permute-start(f32[16,128]{1,0:T(8,128)S(1)} %shard_map.66.refs_0_), channel_id=1, source_target_pairs={{0,2},{2,0},{4,6},{6,4},{8,10},{10,8},{12,14},{14,12},{16,18},{18,... | collective-permute-start | bytes 24584 | tf_op jit(solution)/shard_map/ppermute | solution.py:237
  38.9 0.2 collective-permute-done.10.refs_2_
  39.1 1.9 %collective-permute-done.11.refs_3_ = f32[16,128]{1,0:T(8,128)S(1)} collective-permute-done((f32[16,128]{1,0:T(8,128)S(1)}, f32[16,128]{1,0:T(8,128)S(1)}, u32[]{:S(2)}, u32[]{:S(2)}) %collective-permute-start.11) | collective-permute-done | bytes 8224 | tf_op jit(solution)/shard_map/ppermute | solution.py:237
  41.0 0.0 collective-permute-done.9.refs_1_
  41.0 0.7 %shard_map.67 = (f32[10,32]{1,0:T(8,128)}, f32[3,32]{1,0:T(4,128)}) custom-call(f32[16,128]{1,0:T(8,128)S(1)} %shard_map.66.refs_0_, f32[16,128]{1,0:T(8,128)S(1)} %collective-permute-done.9.refs_1_, f32[16,128]{1,0:T(8,128)S(1)} %collective-permute-done.10.refs_2_, f32[16,128]{1,0:T(8,128)S(1)} %collective-permute-done.11.refs_3_), custom_call_target="tpu_custom_call" | custom-call | bytes 1664 | tf_op jit(solution)/shard_map/pallas_call | solution.py:313
  (5 shorter events, 0.1 us)
Async XLA Ops:
  0.6 1.2 %copy-start = (bf16[512,1024]{1,0:T(8,128)(2,1)S(1)}, bf16[512,1024]{1,0:T(8,128)(2,1)}, u32[]{:S(2)}) copy-start(bf16[512,1024]{1,0:T(8,128)(2,1)} %refs_0_.1) | copy-start | bytes 3145732
  1.9 0.7 %copy-start.3 = (s32[512]{0:T(512)S(1)}, s32[512]{0:T(512)}, u32[]{:S(2)}) copy-start(s32[512]{0:T(512)} %param.7) | copy-start | bytes 6148
  2.5 3.3 %copy-start.2 = (bf16[32,1024]{1,0:T(8,128)(2,1)S(1)}, bf16[32,1024]{1,0:T(8,128)(2,1)}, u32[]{:S(2)}) copy-start(bf16[32,1024]{1,0:T(8,128)(2,1)} %query_ref.1) | copy-start | bytes 196612
  2.6 19.7 %collective-permute-start.2 = (bf16[136,1024]{1,0:T(8,128)(2,1)S(1)}, bf16[136,1024]{1,0:T(8,128)(2,1)S(1)}, u32[]{:S(2)}, u32[]{:S(2)}) collective-permute-start(bf16[136,1024]{1,0:T(8,128)(2,1)S(1)} %get-tuple-element.12), channel_id=1, source_target_pairs={{0,8},{2,10},{4,12},{6,14},{8,0},{10,2},{12,4},{14,6},{16,24},{18,... | collective-permute-start | bytes 835592 | tf_op jit(solution)/shard_map/ppermute | solution.py:237
  5.7 0.7 %copy-start.5 = (s32[32]{0:T(128)S(1)}, s32[32]{0:T(128)}, u32[]{:S(2)}) copy-start(s32[32]{0:T(128)} %param.5) | copy-start | bytes 388
  5.7 16.6 %collective-permute-start = (bf16[128,1024]{1,0:T(8,128)(2,1)S(1)}, bf16[128,1024]{1,0:T(8,128)(2,1)S(1)}, u32[]{:S(2)}, u32[]{:S(2)}) collective-permute-start(bf16[128,1024]{1,0:T(8,128)(2,1)S(1)} %get-tuple-element.11), channel_id=1, source_target_pairs={{0,8},{2,10},{4,12},{6,14},{8,0},{10,2},{12,4},{14,6},{16,24},{18,... | collective-permute-start | bytes 786440 | tf_op jit(solution)/shard_map/ppermute | solution.py:237
  6.4 12.3 %collective-permute-start.4 = (bf16[1,272,128]{2,1,0:T(8,128)(2,1)S(1)}, bf16[1,272,128]{2,1,0:T(8,128)(2,1)S(1)}, u32[]{:S(2)}, u32[]{:S(2)}) collective-permute-start(bf16[1,272,128]{2,1,0:T(8,128)(2,1)S(1)} %shard_map.61), channel_id=1, source_target_pairs={{0,16},{2,18},{4,20},{6,22},{8,24},{10,26},{12,28},{14,30},{16,0},... | collective-permute-start | bytes 208904 | tf_op jit(solution)/shard_map/ppermute | solution.py:237
  18.7 9.6 %copy-start.1 = (bf16[512,1024]{1,0:T(8,128)(2,1)S(1)}, bf16[512,1024]{1,0:T(8,128)(2,1)}, u32[]{:S(2)}) copy-start(bf16[512,1024]{1,0:T(8,128)(2,1)} %refs_0_.1) | copy-start | bytes 3145732
  18.8 9.6 %copy-start.4 = (s32[512]{0:T(512)S(1)}, s32[512]{0:T(512)}, u32[]{:S(2)}) copy-start(s32[512]{0:T(512)} %param.7) | copy-start | bytes 6148
  18.8 6.2 %collective-permute-start.5 = (bf16[2,272,128]{2,1,0:T(8,128)(2,1)S(1)}, bf16[2,272,128]{2,1,0:T(8,128)(2,1)S(1)}, u32[]{:S(2)}, u32[]{:S(2)}) collective-permute-start(bf16[2,272,128]{2,1,0:T(8,128)(2,1)S(1)} %pad_maximum_fusion.refs_3_), channel_id=1, source_target_pairs={{0,2},{2,0},{4,6},{6,4},{8,10},{10,8},{12,14},{14,12},{16,18},{18,... | collective-permute-start | bytes 417800 | tf_op jit(solution)/shard_map/ppermute | solution.py:237
  20.3 8.0 %collective-permute-start.6 = (bf16[2,272,128]{2,1,0:T(8,128)(2,1)S(1)}, bf16[2,272,128]{2,1,0:T(8,128)(2,1)S(1)}, u32[]{:S(2)}, u32[]{:S(2)}) collective-permute-start(bf16[2,272,128]{2,1,0:T(8,128)(2,1)S(1)} %pad_maximum_fusion.refs_3_), channel_id=1, source_target_pairs={{0,4},{2,6},{4,0},{6,2},{8,12},{10,14},{12,8},{14,10},{16,20},{18,... | collective-permute-start | bytes 417800 | tf_op jit(solution)/shard_map/ppermute | solution.py:237
  21.8 6.5 %collective-permute-start.7 = (bf16[2,272,128]{2,1,0:T(8,128)(2,1)S(1)}, bf16[2,272,128]{2,1,0:T(8,128)(2,1)S(1)}, u32[]{:S(2)}, u32[]{:S(2)}) collective-permute-start(bf16[2,272,128]{2,1,0:T(8,128)(2,1)S(1)} %pad_maximum_fusion.refs_3_), channel_id=1, source_target_pairs={{0,6},{2,4},{4,2},{6,0},{8,14},{10,12},{12,10},{14,8},{16,22},{18,... | collective-permute-start | bytes 417800 | tf_op jit(solution)/shard_map/ppermute | solution.py:237
  22.3 7.7 %collective-permute-start.1 = (bf16[128,1024]{1,0:T(8,128)(2,1)S(1)}, bf16[128,1024]{1,0:T(8,128)(2,1)S(1)}, u32[]{:S(2)}, u32[]{:S(2)}) collective-permute-start(bf16[128,1024]{1,0:T(8,128)(2,1)S(1)} %collective-permute-done.refs_0_), channel_id=1, source_target_pairs={{0,1},{1,0},{2,3},{3,2},{4,5},{5,4},{6,7},{7,6},{8,9},{9,8},{10,11... | collective-permute-start | bytes 786440 | tf_op jit(solution)/shard_map/ppermute | solution.py:275
  22.3 6.8 %collective-permute-start.3 = (bf16[136,1024]{1,0:T(8,128)(2,1)S(1)}, bf16[136,1024]{1,0:T(8,128)(2,1)S(1)}, u32[]{:S(2)}, u32[]{:S(2)}) collective-permute-start(bf16[136,1024]{1,0:T(8,128)(2,1)S(1)} %collective-permute-done.2.refs_0_.refs_2_.refs_1_), channel_id=1, source_target_pairs={{0,1},{1,0},{2,3},{3,2},{4,5},{5,4},{6,7},{7,6},{8,9},{9,8},{10,11... | collective-permute-start | bytes 835592 | tf_op jit(solution)/shard_map/ppermute | solution.py:275
  30.4 4.9 %collective-permute-start.8 = (f32[16,128]{1,0:T(8,128)S(1)}, f32[16,128]{1,0:T(8,128)S(1)}, u32[]{:S(2)}, u32[]{:S(2)}) collective-permute-start(f32[16,128]{1,0:T(8,128)S(1)} %get-tuple-element.17), channel_id=1, source_target_pairs={{0,16},{2,18},{4,20},{6,22},{8,24},{10,26},{12,28},{14,30},{16,0},... | collective-permute-start | bytes 24584 | tf_op jit(solution)/shard_map/ppermute | solution.py:237
  35.4 3.7 %collective-permute-start.10 = (f32[16,128]{1,0:T(8,128)S(1)}, f32[16,128]{1,0:T(8,128)S(1)}, u32[]{:S(2)}, u32[]{:S(2)}) collective-permute-start(f32[16,128]{1,0:T(8,128)S(1)} %shard_map.66.refs_0_), channel_id=1, source_target_pairs={{0,4},{2,6},{4,0},{6,2},{8,12},{10,14},{12,8},{14,10},{16,20},{18,... | collective-permute-start | bytes 24584 | tf_op jit(solution)/shard_map/ppermute | solution.py:237
  36.5 4.5 %collective-permute-start.11 = (f32[16,128]{1,0:T(8,128)S(1)}, f32[16,128]{1,0:T(8,128)S(1)}, u32[]{:S(2)}, u32[]{:S(2)}) collective-permute-start(f32[16,128]{1,0:T(8,128)S(1)} %shard_map.66.refs_0_), channel_id=1, source_target_pairs={{0,6},{2,4},{4,2},{6,0},{8,14},{10,12},{12,10},{14,8},{16,22},{18,... | collective-permute-start | bytes 24584 | tf_op jit(solution)/shard_map/ppermute | solution.py:237
  37.3 3.7 %collective-permute-start.9 = (f32[16,128]{1,0:T(8,128)S(1)}, f32[16,128]{1,0:T(8,128)S(1)}, u32[]{:S(2)}, u32[]{:S(2)}) collective-permute-start(f32[16,128]{1,0:T(8,128)S(1)} %shard_map.66.refs_0_), channel_id=1, source_target_pairs={{0,2},{2,0},{4,6},{6,4},{8,10},{10,8},{12,14},{14,12},{16,18},{18,... | collective-permute-start | bytes 24584 | tf_op jit(solution)/shard_map/ppermute | solution.py:237

commit v2 on v1

--- a/solution.py
+++ b/solution.py
@@ -58,24 +58,40 @@
     return jnp.where(row == 0, high, jnp.where(row == 1, low, 0.0)).astype(jnp.bfloat16)
 
 
-def pack_queries(query_ref, wanted_ref, block_ref):
+def prepare(query_hbm, wanted_hbm, ids_hbm, block_ref, digits_ref, state_ref, *refs):
+    query_ref, wanted_ref, ids_ref, sems = refs
     rows, depth = query_ref.shape
     columns = depth // LANES
+    pairs = [(query_hbm, query_ref), (wanted_hbm, wanted_ref), (ids_hbm, ids_ref)]
+    copies = [pltpu.make_async_copy(a, b, sems.at[i]) for i, (a, b) in enumerate(pairs)]
+    for copy in copies:
+        copy.start()
+    for i in range(TOPK + 1):
+        state_ref[i] = jnp.full((8, LANES), -jnp.inf if i < TOPK else 0.0, jnp.float32)
+    for copy in copies:
+        copy.wait()
     for j in range(columns):
         block_ref[0, j * rows : (j + 1) * rows, :] = query_ref[:, j * LANES : (j + 1) * LANES]
     ids = jnp.concatenate([wanted_ref[...], jnp.zeros((1, LANES - rows), jnp.int32)], axis=1)
     block_ref[0, columns * rows :, :] = digits_of(ids)
-
-
-def pack_texts(text_ref, ids_ref, *part_refs):
-    part, depth = part_refs[-1].shape[0] - (8 if len(part_refs) == 1 else 0), text_ref.shape[1]
-    half = part * len(part_refs)
+    digits_ref[...] = digits_of(ids_ref[...])
+
+
+def pack_texts(text_ref, digits_ref, *part_refs):
+    part, depth = part_refs[-1].shape
+    columns = depth // LANES
+    half = part * PARTS
     start = pl.multiple_of(lax.rem(lax.axis_index("query"), 2) * half, half)
-    for n, part_ref in enumerate(part_refs):
-        part_ref[:part, :] = text_ref[pl.ds(pl.multiple_of(start + n * part, part), part), :]
-    first_ref = part_refs[0]
-    first_ref[part:, :half] = digits_of(ids_ref[:, pl.ds(start, half)])[:8]
-    first_ref[part:, half:] = jnp.zeros((8, depth - half), jnp.bfloat16)
+    for j in range(columns):
+        lanes = slice(j * LANES, (j + 1) * LANES)
+        part_refs[0][j * part : (j + 1) * part, :] = text_ref[pl.ds(start, part), lanes]
+    spot = columns * part
+    digits = digits_ref[:8, pl.ds(start, half)]
+    for n in range(half // LANES):
+        lanes = slice(n * LANES, (n + 1) * LANES)
+        part_refs[0][spot + 8 * n : spot + 8 * n + 8, :] = digits[:, lanes]
+    for n in range(1, PARTS):
+        part_refs[n][...] = text_ref[pl.ds(pl.multiple_of(start + n * part, part), part), :]
 
 
 def scan(text_ref, queries, label_ref, score_ref, wanted, states):
@@ -116,16 +132,11 @@
     return digits[0:1] * 256.0 + digits[1:2]
 
 
-def blank(state_ref):
-    for i in range(TOPK + 1):
-        state_ref[i] = jnp.full((8, LANES), -jnp.inf if i < TOPK else 0.0, jnp.float32)
-
-
 def rank_own(*refs, tiles, rows):
     text_ref, ids_ref, blank_ref = refs[:3]
     refs = refs[1:]
-    bundles = refs[2 : 2 + PLANE]
-    query_ref, wanted_ref, state_ref, score_ref, label_ref = refs[2 + PLANE :]
+    blocks, rests = refs[2 : 2 + PLANE], refs[2 + PLANE : 2 + 2 * PLANE]
+    query_ref, wanted_ref, state_ref, score_ref, label_ref = refs[2 + 2 * PLANE :]
     columns = text_ref.shape[1] // LANES
     spread(ids_ref[...].astype(jnp.float32), label_ref)
     wanted = []
@@ -133,7 +144,7 @@
         total = jnp.zeros((1, LANES), jnp.float32)
         for d in range(PLANE):
             at = slice(h * LANES + d * rows, h * LANES + (d + 1) * rows)
-            source = bundles[d].at[h]
+            source = blocks[d].at[0] if h == 0 else rests[d].at[h - 1]
             for j in range(columns):
                 query_ref[at, j * LANES : (j + 1) * LANES] = source[j * rows : (j + 1) * rows, :]
             here = joined(source[columns * rows :, :])
@@ -153,21 +164,28 @@
     return wanted, [[state_ref[h, i] for i in range(TOPK + 1)] for h in range(tiles)]
 
 
-def scan_part(part_ref, first_ref, count, query_ref, wanted, states, score_ref, label_ref, part):
-    at = slice(part * count, (part + 1) * count)
-    spread(joined(first_ref[count:, at]), label_ref)
+def scan_part(part_ref, first_ref, text_ref, query_ref, wanted, states, score_ref, label_ref, part):
+    count, depth = text_ref.shape
+    columns = depth // LANES
+    for n in range(count // LANES):
+        at = columns * count + 8 * (part * (count // LANES) + n)
+        spread(joined(first_ref[at : at + 8, :]), label_ref.at[pl.ds(n * LANES, LANES)])
+    if part == 0:
+        for j in range(columns):
+            lanes = slice(j * LANES, (j + 1) * LANES)
+            text_ref[:, lanes] = part_ref[j * count : (j + 1) * count, :]
+        part_ref = text_ref
     return scan(part_ref, query_ref[...], label_ref, score_ref, wanted, states)
 
 
 def rank_parts(*refs, parts):
     part_refs, refs = refs[: len(parts)], refs[len(parts) :]
     first_refs, refs = refs[: len(parts)], refs[len(parts) :]
-    query_ref, wanted_ref, state_ref, next_ref, score_ref, label_ref = refs
-    count = score_ref.shape[0]
+    query_ref, wanted_ref, state_ref, next_ref, score_ref, label_ref, text_ref = refs
     wanted, states = load_states(wanted_ref, state_ref)
     for part_ref, first_ref, part in zip(part_refs, first_refs, parts):
         states = scan_part(
-            part_ref, first_ref, count, query_ref, wanted, states, score_ref, label_ref, part
+            part_ref, first_ref, text_ref, query_ref, wanted, states, score_ref, label_ref, part
         )
     for h, state in enumerate(states):
         for i in range(TOPK + 1):
@@ -175,11 +193,10 @@
 
 
 def rank_last(part_ref, first_ref, query_ref, wanted_ref, state_ref, *refs, part):
-    outs, (score_ref, label_ref) = refs[:-2], refs[-2:]
-    count = score_ref.shape[0]
+    outs, (score_ref, label_ref, text_ref) = refs[:-3], refs[-3:]
     wanted, states = load_states(wanted_ref, state_ref)
     states = scan_part(
-        part_ref, first_ref, count, query_ref, wanted, states, score_ref, label_ref, part
+        part_ref, first_ref, text_ref, query_ref, wanted, states, score_ref, label_ref, part
     )
     for out_ref, state in zip(outs, states):
         best, truth = list(state[:TOPK]), state[TOPK]
@@ -237,24 +254,44 @@
         return lax.ppermute(x, "text", [(i, i ^ s) for i in range(texts)])
 
     packed = (depth // LANES) * rows + 16
-    pack = kernel(pack_queries, jax.ShapeDtypeStruct((1, packed, LANES), bf16), 1)
-    empty = kernel(blank, jax.ShapeDtypeStruct((TOPK + 1, 8, LANES), f32), 1, flops=4 * 10**9)()
-    bundle = pack(query_embed, truth_ids.reshape(1, rows))
     part = own // 2 // PARTS
+    inputs = (query_embed, truth_ids.reshape(1, rows), text_ids.reshape(1, own))
+    block, digits, empty = kernel(
+        prepare,
+        [
+            jax.ShapeDtypeStruct((1, packed, LANES), bf16),
+            jax.ShapeDtypeStruct((16, own), bf16),
+            jax.ShapeDtypeStruct((TOPK + 1, 8, LANES), f32),
+        ],
+        1,
+        flops=4 * 10**9,
+        in_specs=[pl.BlockSpec(memory_space=pltpu.HBM)] * 3,
+        scratch_shapes=[
+            pltpu.VMEM((rows, depth), bf16),
+            pltpu.VMEM((1, rows), jnp.int32),
+            pltpu.VMEM((1, own), jnp.int32),
+            pltpu.SemaphoreType.DMA((3,)),
+        ],
+    )(*[pltpu.with_memory_space_constraint(x, pltpu.HBM) for x in inputs])
+    first_rows = (depth // LANES) * part + 8 * (own // 2 // LANES)
     sent = kernel(
         pack_texts,
-        [jax.ShapeDtypeStruct((part + (8 if n == 0 else 0), depth), bf16) for n in range(PARTS)],
+        [jax.ShapeDtypeStruct((first_rows, LANES), bf16)]
+        + [jax.ShapeDtypeStruct((part, depth), bf16)] * (PARTS - 1),
         1,
-    )(text_embed, text_ids.reshape(1, own))
+    )(text_embed, digits)
     near = [permute(x, PAIR) for x in sent]
-    far_bits = []
-    s = 2 * PAIR
+    blocks = [block] + [permute(block, d) for d in range(1, PLANE)]
+    far_bits = [2 * PAIR]
+    rest = permute(block, 2 * PAIR)
+    s = 4 * PAIR
     while s < texts:
-        bundle = jnp.concatenate([bundle, permute(bundle, s)], axis=0)
+        new, more = permute(block, s), permute(rest, s)
+        rest = jnp.concatenate([rest, new, more], axis=0)
         far_bits.append(s)
         s *= 2
-    tiles = bundle.shape[0]
-    bundles = [bundle] + [permute(bundle, d) for d in range(1, PLANE)]
+    tiles = 1 + rest.shape[0]
+    rests = [rest] + [permute(rest, d) for d in range(1, PLANE)]
 
     state_shape = jax.ShapeDtypeStruct((tiles, TOPK + 1, 8, LANES), f32)
     list_shape = jax.ShapeDtypeStruct((16, LANES), f32)
@@ -269,11 +306,15 @@
         12,
         flops=flops,
         scratch_shapes=[pltpu.VMEM((own, tiles * LANES), f32), pltpu.VMEM((own, LANES), f32)],
-    )(text_embed, text_ids.reshape(1, own), empty, *bundles)
+    )(text_embed, text_ids.reshape(1, own), empty, *blocks, *rests)
     far = []
     for x in near:
         far.append(lax.ppermute(x, "query", [(i, i ^ 1) for i in range(cores)]))
-    scratch = [pltpu.VMEM((part, tiles * LANES), f32), pltpu.VMEM((part, LANES), f32)]
+    scratch = [
+        pltpu.VMEM((part, tiles * LANES), f32),
+        pltpu.VMEM((part, LANES), f32),
+        pltpu.VMEM((part, depth), bf16),
+    ]
     flops = flops // 2 // PARTS
 
     def rank(parts):

time: 42 us -> 49.1 us (1.17)
  waiting for transfers between devices: 18.9 us -> 25.1 us
  starting transfers between devices: 16.8 us -> 19 us
  local copies, waits for them, and re-layouts: 2.48 us -> 0.3 us
  Pallas kernels: 2.85 us -> 3.87 us
    ppermute x10 -> x13, waiting for transfers between devices: 18.9 us -> 25.1 us  [permute(): return lax.ppermute(x, 'text', [(i, i ^ s) for i in range(texts)])]
    ppermute x10 -> x13, starting transfers between devices: 16.3 us -> 19 us  [permute(): return lax.ppermute(x, 'text', [(i, i ^ s) for i in range(texts)])]
    unnamed x12 -> x4, local copies, waits for them, and re-layouts: 2.48 us -> 0.3 us
    pallas_call x3 -> x2, Pallas kernels: 0.06 us -> 1.04 us  [the longest x1 0.98 us: per_device(): kernel(prepare, [jax.ShapeDtypeStruct((1, packed, LANES), bf16), jax.Shap...]
    ppermute x2, starting transfers between devices: 0.51 us -> 0.01 us  [per_device(): far.append(lax.ppermute(x, 'query', [(i, i ^ 1) for i in range(cores)]))]
  transfers between devices with their start and end apart: 12 -> 15, of which waited for: 6 -> 10; matrix products, arithmetic and copies ran while one was open for 0% -> 0% of each run, Pallas kernels for 4% -> 4%
where the time goes in v2:
time: 49.1 us; the launch traced here: 49 us
  waiting for transfers between devices  25.1 us (51%)
  starting transfers between devices  19 us (39%)
  Pallas kernels  3.87 us (8%)
  between operations  0.71 us (1%)
    ppermute x13, waiting for transfers between devices, permute(): return lax.ppermute(x, 'text', [(i, i ^ s) for i in range(texts)])  25.1 us
    ppermute x13, starting transfers between devices, permute(): return lax.ppermute(x, 'text', [(i, i ^ s) for i in range(texts)])  19 us
  transfers between devices with their start and end apart: 15, of which 10 were waited for; matrix products, arithmetic and copies ran while one was open for 0% of the time, Pallas kernels for 4%

profile of v2, /device:TPU:0, one launch (start us, length us, event | category | flops | bytes accessed | tf_op | source)
XLA Modules:
  0.0 49.0 jit_solution(13804403576666484796)
XLA Ops:
  0.6 0.0 copy-start
  0.6 1.0 %shard_map.59 = (bf16[1,272,128]{2,1,0:T(8,128)(2,1)S(1)}, bf16[16,512]{1,0:T(8,128)(2,1)S(1)}, f32[11,8,128]{2,1,0:T(8,128)S(1)}) custom-call(bf16[32,1024]{1,0:T(8,128)(2,1)} %query_hbm.1, s32[1,32]{1,0:T(1,128)} %bitcast.8, s32[1,512]{1,0:T(1,128)} %bitcast.4), custom_call_target="tpu_custom_call" | custom-call | flops 4000000000 | bytes 131072 | tf_op jit(solution)/shard_map/pallas_call | solution.py:259
  1.6 0.3 copy-done
  1.9 0.1 shard_map.60
  2.0 3.1 %collective-permute-start.2 = (bf16[1040,128]{1,0:T(8,128)(2,1)S(1)}, bf16[1040,128]{1,0:T(8,128)(2,1)S(1)}, u32[]{:S(2)}, u32[]{:S(2)}) collective-permute-start(bf16[1040,128]{1,0:T(8,128)(2,1)S(1)} %get-tuple-element.16), channel_id=1, source_target_pairs={{0,8},{2,10},{4,12},{6,14},{8,0},{10,2},{12,4},{14,6},{16,24},{18,... | collective-permute-start | bytes 798728 | tf_op jit(solution)/shard_map/ppermute | solution.py:254
  5.1 0.0 copy-start.1
  5.1 0.1 collective-permute-start
  5.2 7.2 %collective-permute-done.2.refs_0_.refs_2_.refs_1_ = bf16[1040,128]{1,0:T(8,128)(2,1)S(1)} collective-permute-done((bf16[1040,128]{1,0:T(8,128)(2,1)S(1)}, bf16[1040,128]{1,0:T(8,128)(2,1)S(1)}, u32[]{:S(2)}, u32[]{:S(2)}) %collective-permute-start.2) | collective-permute-done | bytes 266272 | tf_op jit(solution)/shard_map/ppermute | solution.py:254
  12.3 0.0 collective-permute-start.3
  12.3 4.8 %collective-permute-done.refs_0_ = bf16[128,1024]{1,0:T(8,128)(2,1)S(1)} collective-permute-done((bf16[128,1024]{1,0:T(8,128)(2,1)S(1)}, bf16[128,1024]{1,0:T(8,128)(2,1)S(1)}, u32[]{:S(2)}, u32[]{:S(2)}) %collective-permute-start) | collective-permute-done | bytes 262176 | tf_op jit(solution)/shard_map/ppermute | solution.py:254
  17.1 0.0 collective-permute-start.1
  17.1 2.8 %collective-permute-start.7 = (bf16[1,272,128]{2,1,0:T(8,128)(2,1)S(1)}, bf16[1,272,128]{2,1,0:T(8,128)(2,1)S(1)}, u32[]{:S(2)}, u32[]{:S(2)}) collective-permute-start(bf16[1,272,128]{2,1,0:T(8,128)(2,1)S(1)} %get-tuple-element.18.refs_3_), channel_id=1, source_target_pairs={{0,16},{2,18},{4,20},{6,22},{8,24},{10,26},{12,28},{14,30},{16,0},... | collective-permute-start | bytes 208904 | tf_op jit(solution)/shard_map/ppermute | solution.py:254
  19.9 1.5 %collective-permute-start.4 = (bf16[1,272,128]{2,1,0:T(8,128)(2,1)S(1)}, bf16[1,272,128]{2,1,0:T(8,128)(2,1)S(1)}, u32[]{:S(2)}, u32[]{:S(2)}) collective-permute-start(bf16[1,272,128]{2,1,0:T(8,128)(2,1)S(1)} %get-tuple-element.18.refs_3_), channel_id=1, source_target_pairs={{0,2},{2,0},{4,6},{6,4},{8,10},{10,8},{12,14},{14,12},{16,18},{18,... | collective-permute-start | bytes 208904 | tf_op jit(solution)/shard_map/ppermute | solution.py:254
  21.4 1.5 %collective-permute-start.5 = (bf16[1,272,128]{2,1,0:T(8,128)(2,1)S(1)}, bf16[1,272,128]{2,1,0:T(8,128)(2,1)S(1)}, u32[]{:S(2)}, u32[]{:S(2)}) collective-permute-start(bf16[1,272,128]{2,1,0:T(8,128)(2,1)S(1)} %get-tuple-element.18.refs_3_), channel_id=1, source_target_pairs={{0,4},{2,6},{4,0},{6,2},{8,12},{10,14},{12,8},{14,10},{16,20},{18,... | collective-permute-start | bytes 208904 | tf_op jit(solution)/shard_map/ppermute | solution.py:254
  22.9 1.3 %collective-permute-done.7.refs_7_ = bf16[1,272,128]{2,1,0:T(8,128)(2,1)S(1)} collective-permute-done((bf16[1,272,128]{2,1,0:T(8,128)(2,1)S(1)}, bf16[1,272,128]{2,1,0:T(8,128)(2,1)S(1)}, u32[]{:S(2)}, u32[]{:S(2)}) %collective-permute-start.7) | collective-permute-done | bytes 69664 | tf_op jit(solution)/shard_map/ppermute | solution.py:254
  24.2 2.5 %collective-permute-start.6 = (bf16[1,272,128]{2,1,0:T(8,128)(2,1)S(1)}, bf16[1,272,128]{2,1,0:T(8,128)(2,1)S(1)}, u32[]{:S(2)}, u32[]{:S(2)}) collective-permute-start(bf16[1,272,128]{2,1,0:T(8,128)(2,1)S(1)} %get-tuple-element.18.refs_3_), channel_id=1, source_target_pairs={{0,6},{2,4},{4,2},{6,0},{8,14},{10,12},{12,10},{14,8},{16,22},{18,... | collective-permute-start | bytes 208904 | tf_op jit(solution)/shard_map/ppermute | solution.py:254
  26.7 0.0 collective-permute-done.4.refs_4_
  26.7 0.4 collective-permute-start.10
  27.1 0.0 collective-permute-done.5.refs_5_
  27.1 1.5 %collective-permute-start.8 = (bf16[1,272,128]{2,1,0:T(8,128)(2,1)S(1)}, bf16[1,272,128]{2,1,0:T(8,128)(2,1)S(1)}, u32[]{:S(2)}, u32[]{:S(2)}) collective-permute-start(bf16[1,272,128]{2,1,0:T(8,128)(2,1)S(1)} %collective-permute-done.7.refs_7_), channel_id=1, source_target_pairs={{0,2},{2,0},{4,6},{6,4},{8,10},{10,8},{12,14},{14,12},{16,18},{18,... | collective-permute-start | bytes 208904 | tf_op jit(solution)/shard_map/ppermute | solution.py:254
  28.7 1.5 %collective-permute-done.6.refs_6_ = bf16[1,272,128]{2,1,0:T(8,128)(2,1)S(1)} collective-permute-done((bf16[1,272,128]{2,1,0:T(8,128)(2,1)S(1)}, bf16[1,272,128]{2,1,0:T(8,128)(2,1)S(1)}, u32[]{:S(2)}, u32[]{:S(2)}) %collective-permute-start.6) | collective-permute-done | bytes 69664 | tf_op jit(solution)/shard_map/ppermute | solution.py:254
  30.2 1.2 %collective-permute-start.9 = (bf16[1,272,128]{2,1,0:T(8,128)(2,1)S(1)}, bf16[1,272,128]{2,1,0:T(8,128)(2,1)S(1)}, u32[]{:S(2)}, u32[]{:S(2)}) collective-permute-start(bf16[1,272,128]{2,1,0:T(8,128)(2,1)S(1)} %collective-permute-done.7.refs_7_), channel_id=1, source_target_pairs={{0,4},{2,6},{4,0},{6,2},{8,12},{10,14},{12,8},{14,10},{16,20},{18,... | collective-permute-start | bytes 208904 | tf_op jit(solution)/shard_map/ppermute | solution.py:254
  31.4 0.6 %collective-permute-done.10.refs_10_ = bf16[1,272,128]{2,1,0:T(8,128)(2,1)S(1)} collective-permute-done((bf16[1,272,128]{2,1,0:T(8,128)(2,1)S(1)}, bf16[1,272,128]{2,1,0:T(8,128)(2,1)S(1)}, u32[]{:S(2)}, u32[]{:S(2)}) %collective-permute-start.10) | collective-permute-done | bytes 69664 | tf_op jit(solution)/shard_map/ppermute | solution.py:254
  31.9 0.0 collective-permute-done.8.refs_8_
  31.9 2.5 %collective-permute-done.9.refs_9_ = bf16[1,272,128]{2,1,0:T(8,128)(2,1)S(1)} collective-permute-done((bf16[1,272,128]{2,1,0:T(8,128)(2,1)S(1)}, bf16[1,272,128]{2,1,0:T(8,128)(2,1)S(1)}, u32[]{:S(2)}, u32[]{:S(2)}) %collective-permute-start.9) | collective-permute-done | bytes 69664 | tf_op jit(solution)/shard_map/ppermute | solution.py:254
  34.5 0.0 copy-done.1
  34.5 0.8 %shard_map.61 = (bf16[256,1024]{1,0:T(8,128)(2,1)S(1)}, f32[2,8,128]{2,1,0:T(8,128)S(1)}, f32[2,11,8,128]{3,2,1,0:T(8,128)S(1)}) custom-call(bf16[512,1024]{1,0:T(8,128)(2,1)S(1)} %copy-done, s32[1,512]{1,0:T(1,128)S(1)} %bitcast.5, f32[11,8,128]{2,1,0:T(8,128)S(1)} %get-tuple-element.17.refs_2_, bf16[1,272,128]{2,1,0:T(8,128)(2,1)S(1)} %get-tuple-element.18.refs_3_, ...), custom_call_target="tpu_custom_call" | custom-call | flops 268435456 | bytes 622592 | tf_op jit(solution)/shard_map/pallas_call | solution.py:299
  35.3 0.0 collective-permute-done.3.refs_1_.refs_3_
  35.3 0.6 %shard_map.62.refs_4_ = f32[2,11,8,128]{3,2,1,0:T(8,128)S(1)} custom-call(bf16[1040,128]{1,0:T(8,128)(2,1)S(1)} %collective-permute-done.2.refs_0_.refs_2_.refs_1_, bf16[1040,128]{1,0:T(8,128)(2,1)S(1)} %collective-permute-done.3.refs_1_.refs_3_, bf16[1040,128]{1,0:T(8,128)(2,1)S(1)} %collective-permute-done.2.refs_0_.refs_2_.refs_1_, ...), custom_call_target="tpu_custom_call" | custom-call | flops 134217728 | bytes 90112 | tf_op jit(solution)/shard_map/pallas_call | solution.py:321
  35.9 0.3 shard_map.63.refs_4_
  36.3 0.0 collective-permute-done.1.refs_0_
  36.3 0.4 shard_map.64
  36.7 0.8 %collective-permute-start.11 = (f32[16,128]{1,0:T(8,128)S(1)}, f32[16,128]{1,0:T(8,128)S(1)}, u32[]{:S(2)}, u32[]{:S(2)}) collective-permute-start(f32[16,128]{1,0:T(8,128)S(1)} %get-tuple-element.23), channel_id=1, source_target_pairs={{0,16},{2,18},{4,20},{6,22},{8,24},{10,26},{12,28},{14,30},{16,0},... | collective-permute-start | bytes 24584 | tf_op jit(solution)/shard_map/ppermute | solution.py:254
  37.5 3.8 %collective-permute-done.11.theirs_ref = f32[16,128]{1,0:T(8,128)S(1)} collective-permute-done((f32[16,128]{1,0:T(8,128)S(1)}, f32[16,128]{1,0:T(8,128)S(1)}, u32[]{:S(2)}, u32[]{:S(2)}) %collective-permute-start.11) | collective-permute-done | bytes 8224 | tf_op jit(solution)/shard_map/ppermute | solution.py:254
  41.3 1.3 %collective-permute-start.12 = (f32[16,128]{1,0:T(8,128)S(1)}, f32[16,128]{1,0:T(8,128)S(1)}, u32[]{:S(2)}, u32[]{:S(2)}) collective-permute-start(f32[16,128]{1,0:T(8,128)S(1)} %shard_map.65.refs_0_), channel_id=1, source_target_pairs={{0,2},{2,0},{4,6},{6,4},{8,10},{10,8},{12,14},{14,12},{16,18},{18,... | collective-permute-start | bytes 24584 | tf_op jit(solution)/shard_map/ppermute | solution.py:254
  42.6 1.1 %collective-permute-start.13 = (f32[16,128]{1,0:T(8,128)S(1)}, f32[16,128]{1,0:T(8,128)S(1)}, u32[]{:S(2)}, u32[]{:S(2)}) collective-permute-start(f32[16,128]{1,0:T(8,128)S(1)} %shard_map.65.refs_0_), channel_id=1, source_target_pairs={{0,4},{2,6},{4,0},{6,2},{8,12},{10,14},{12,8},{14,10},{16,20},{18,... | collective-permute-start | bytes 24584 | tf_op jit(solution)/shard_map/ppermute | solution.py:254
  43.7 1.1 %collective-permute-start.14 = (f32[16,128]{1,0:T(8,128)S(1)}, f32[16,128]{1,0:T(8,128)S(1)}, u32[]{:S(2)}, u32[]{:S(2)}) collective-permute-start(f32[16,128]{1,0:T(8,128)S(1)} %shard_map.65.refs_0_), channel_id=1, source_target_pairs={{0,6},{2,4},{4,2},{6,0},{8,14},{10,12},{12,10},{14,8},{16,22},{18,... | collective-permute-start | bytes 24584 | tf_op jit(solution)/shard_map/ppermute | solution.py:254
  44.8 0.2 collective-permute-done.12.refs_1_
  45.0 1.3 %collective-permute-done.13.refs_2_ = f32[16,128]{1,0:T(8,128)S(1)} collective-permute-done((f32[16,128]{1,0:T(8,128)S(1)}, f32[16,128]{1,0:T(8,128)S(1)}, u32[]{:S(2)}, u32[]{:S(2)}) %collective-permute-start.13) | collective-permute-done | bytes 8224 | tf_op jit(solution)/shard_map/ppermute | solution.py:254
  46.3 2.0 %collective-permute-done.14.refs_3_ = f32[16,128]{1,0:T(8,128)S(1)} collective-permute-done((f32[16,128]{1,0:T(8,128)S(1)}, f32[16,128]{1,0:T(8,128)S(1)}, u32[]{:S(2)}, u32[]{:S(2)}) %collective-permute-start.14) | collective-permute-done | bytes 8224 | tf_op jit(solution)/shard_map/ppermute | solution.py:254
  48.3 0.7 %shard_map.66 = (f32[10,32]{1,0:T(8,128)}, f32[3,32]{1,0:T(4,128)}) custom-call(f32[16,128]{1,0:T(8,128)S(1)} %shard_map.65.refs_0_, f32[16,128]{1,0:T(8,128)S(1)} %collective-permute-done.12.refs_1_, f32[16,128]{1,0:T(8,128)S(1)} %collective-permute-done.13.refs_2_, f32[16,128]{1,0:T(8,128)S(1)} %collective-permute-done.14.refs_3_), custom_call_target="tpu_custom_call" | custom-call | bytes 1664 | tf_op jit(solution)/shard_map/pallas_call | solution.py:354
  (1 shorter events, 0.0 us)
Async XLA Ops:
  0.6 1.3 %copy-start = (bf16[512,1024]{1,0:T(8,128)(2,1)S(1)}, bf16[512,1024]{1,0:T(8,128)(2,1)}, u32[]{:S(2)}) copy-start(bf16[512,1024]{1,0:T(8,128)(2,1)} %refs_0_.1) | copy-start | bytes 3145732
  2.0 10.4 %collective-permute-start.2 = (bf16[1040,128]{1,0:T(8,128)(2,1)S(1)}, bf16[1040,128]{1,0:T(8,128)(2,1)S(1)}, u32[]{:S(2)}, u32[]{:S(2)}) collective-permute-start(bf16[1040,128]{1,0:T(8,128)(2,1)S(1)} %get-tuple-element.16), channel_id=1, source_target_pairs={{0,8},{2,10},{4,12},{6,14},{8,0},{10,2},{12,4},{14,6},{16,24},{18,... | collective-permute-start | bytes 798728 | tf_op jit(solution)/shard_map/ppermute | solution.py:254
  5.1 29.4 %copy-start.1 = (s32[512]{0:T(512)S(1)}, s32[512]{0:T(512)}, u32[]{:S(2)}) copy-start(s32[512]{0:T(512)} %param.7) | copy-start | bytes 6148
  5.1 12.0 %collective-permute-start = (bf16[128,1024]{1,0:T(8,128)(2,1)S(1)}, bf16[128,1024]{1,0:T(8,128)(2,1)S(1)}, u32[]{:S(2)}, u32[]{:S(2)}) collective-permute-start(bf16[128,1024]{1,0:T(8,128)(2,1)S(1)} %get-tuple-element.15), channel_id=1, source_target_pairs={{0,8},{2,10},{4,12},{6,14},{8,0},{10,2},{12,4},{14,6},{16,24},{18,... | collective-permute-start | bytes 786440 | tf_op jit(solution)/shard_map/ppermute | solution.py:254
  12.3 22.9 %collective-permute-start.3 = (bf16[1040,128]{1,0:T(8,128)(2,1)S(1)}, bf16[1040,128]{1,0:T(8,128)(2,1)S(1)}, u32[]{:S(2)}, u32[]{:S(2)}) collective-permute-start(bf16[1040,128]{1,0:T(8,128)(2,1)S(1)} %collective-permute-done.2.refs_0_.refs_2_.refs_1_), channel_id=1, source_target_pairs={{0,1},{1,0},{2,3},{3,2},{4,5},{5,4},{6,7},{7,6},{8,9},{9,8},{10,11... | collective-permute-start | bytes 798728 | tf_op jit(solution)/shard_map/ppermute | solution.py:312
  17.1 19.1 %collective-permute-start.1 = (bf16[128,1024]{1,0:T(8,128)(2,1)S(1)}, bf16[128,1024]{1,0:T(8,128)(2,1)S(1)}, u32[]{:S(2)}, u32[]{:S(2)}) collective-permute-start(bf16[128,1024]{1,0:T(8,128)(2,1)S(1)} %collective-permute-done.refs_0_), channel_id=1, source_target_pairs={{0,1},{1,0},{2,3},{3,2},{4,5},{5,4},{6,7},{7,6},{8,9},{9,8},{10,11... | collective-permute-start | bytes 786440 | tf_op jit(solution)/shard_map/ppermute | solution.py:312
  17.1 7.1 %collective-permute-start.7 = (bf16[1,272,128]{2,1,0:T(8,128)(2,1)S(1)}, bf16[1,272,128]{2,1,0:T(8,128)(2,1)S(1)}, u32[]{:S(2)}, u32[]{:S(2)}) collective-permute-start(bf16[1,272,128]{2,1,0:T(8,128)(2,1)S(1)} %get-tuple-element.18.refs_3_), channel_id=1, source_target_pairs={{0,16},{2,18},{4,20},{6,22},{8,24},{10,26},{12,28},{14,30},{16,0},... | collective-permute-start | bytes 208904 | tf_op jit(solution)/shard_map/ppermute | solution.py:254
  19.9 6.8 %collective-permute-start.4 = (bf16[1,272,128]{2,1,0:T(8,128)(2,1)S(1)}, bf16[1,272,128]{2,1,0:T(8,128)(2,1)S(1)}, u32[]{:S(2)}, u32[]{:S(2)}) collective-permute-start(bf16[1,272,128]{2,1,0:T(8,128)(2,1)S(1)} %get-tuple-element.18.refs_3_), channel_id=1, source_target_pairs={{0,2},{2,0},{4,6},{6,4},{8,10},{10,8},{12,14},{14,12},{16,18},{18,... | collective-permute-start | bytes 208904 | tf_op jit(solution)/shard_map/ppermute | solution.py:254
  21.4 5.8 %collective-permute-start.5 = (bf16[1,272,128]{2,1,0:T(8,128)(2,1)S(1)}, bf16[1,272,128]{2,1,0:T(8,128)(2,1)S(1)}, u32[]{:S(2)}, u32[]{:S(2)}) collective-permute-start(bf16[1,272,128]{2,1,0:T(8,128)(2,1)S(1)} %get-tuple-element.18.refs_3_), channel_id=1, source_target_pairs={{0,4},{2,6},{4,0},{6,2},{8,12},{10,14},{12,8},{14,10},{16,20},{18,... | collective-permute-start | bytes 208904 | tf_op jit(solution)/shard_map/ppermute | solution.py:254
  24.2 6.0 %collective-permute-start.6 = (bf16[1,272,128]{2,1,0:T(8,128)(2,1)S(1)}, bf16[1,272,128]{2,1,0:T(8,128)(2,1)S(1)}, u32[]{:S(2)}, u32[]{:S(2)}) collective-permute-start(bf16[1,272,128]{2,1,0:T(8,128)(2,1)S(1)} %get-tuple-element.18.refs_3_), channel_id=1, source_target_pairs={{0,6},{2,4},{4,2},{6,0},{8,14},{10,12},{12,10},{14,8},{16,22},{18,... | collective-permute-start | bytes 208904 | tf_op jit(solution)/shard_map/ppermute | solution.py:254
  26.7 5.2 %collective-permute-start.10 = (bf16[1,272,128]{2,1,0:T(8,128)(2,1)S(1)}, bf16[1,272,128]{2,1,0:T(8,128)(2,1)S(1)}, u32[]{:S(2)}, u32[]{:S(2)}) collective-permute-start(bf16[1,272,128]{2,1,0:T(8,128)(2,1)S(1)} %collective-permute-done.7.refs_7_), channel_id=1, source_target_pairs={{0,6},{2,4},{4,2},{6,0},{8,14},{10,12},{12,10},{14,8},{16,22},{18,... | collective-permute-start | bytes 208904 | tf_op jit(solution)/shard_map/ppermute | solution.py:254
  27.1 4.8 %collective-permute-start.8 = (bf16[1,272,128]{2,1,0:T(8,128)(2,1)S(1)}, bf16[1,272,128]{2,1,0:T(8,128)(2,1)S(1)}, u32[]{:S(2)}, u32[]{:S(2)}) collective-permute-start(bf16[1,272,128]{2,1,0:T(8,128)(2,1)S(1)} %collective-permute-done.7.refs_7_), channel_id=1, source_target_pairs={{0,2},{2,0},{4,6},{6,4},{8,10},{10,8},{12,14},{14,12},{16,18},{18,... | collective-permute-start | bytes 208904 | tf_op jit(solution)/shard_map/ppermute | solution.py:254
  30.2 4.3 %collective-permute-start.9 = (bf16[1,272,128]{2,1,0:T(8,128)(2,1)S(1)}, bf16[1,272,128]{2,1,0:T(8,128)(2,1)S(1)}, u32[]{:S(2)}, u32[]{:S(2)}) collective-permute-start(bf16[1,272,128]{2,1,0:T(8,128)(2,1)S(1)} %collective-permute-done.7.refs_7_), channel_id=1, source_target_pairs={{0,4},{2,6},{4,0},{6,2},{8,12},{10,14},{12,8},{14,10},{16,20},{18,... | collective-permute-start | bytes 208904 | tf_op jit(solution)/shard_map/ppermute | solution.py:254
  36.7 4.6 %collective-permute-start.11 = (f32[16,128]{1,0:T(8,128)S(1)}, f32[16,128]{1,0:T(8,128)S(1)}, u32[]{:S(2)}, u32[]{:S(2)}) collective-permute-start(f32[16,128]{1,0:T(8,128)S(1)} %get-tuple-element.23), channel_id=1, source_target_pairs={{0,16},{2,18},{4,20},{6,22},{8,24},{10,26},{12,28},{14,30},{16,0},... | collective-permute-start | bytes 24584 | tf_op jit(solution)/shard_map/ppermute | solution.py:254
  41.3 3.7 %collective-permute-start.12 = (f32[16,128]{1,0:T(8,128)S(1)}, f32[16,128]{1,0:T(8,128)S(1)}, u32[]{:S(2)}, u32[]{:S(2)}) collective-permute-start(f32[16,128]{1,0:T(8,128)S(1)} %shard_map.65.refs_0_), channel_id=1, source_target_pairs={{0,2},{2,0},{4,6},{6,4},{8,10},{10,8},{12,14},{14,12},{16,18},{18,... | collective-permute-start | bytes 24584 | tf_op jit(solution)/shard_map/ppermute | solution.py:254
  42.6 3.7 %collective-permute-start.13 = (f32[16,128]{1,0:T(8,128)S(1)}, f32[16,128]{1,0:T(8,128)S(1)}, u32[]{:S(2)}, u32[]{:S(2)}) collective-permute-start(f32[16,128]{1,0:T(8,128)S(1)} %shard_map.65.refs_0_), channel_id=1, source_target_pairs={{0,4},{2,6},{4,0},{6,2},{8,12},{10,14},{12,8},{14,10},{16,20},{18,... | collective-permute-start | bytes 24584 | tf_op jit(solution)/shard_map/ppermute | solution.py:254
  43.7 4.5 %collective-permute-start.14 = (f32[16,128]{1,0:T(8,128)S(1)}, f32[16,128]{1,0:T(8,128)S(1)}, u32[]{:S(2)}, u32[]{:S(2)}) collective-permute-start(f32[16,128]{1,0:T(8,128)S(1)} %shard_map.65.refs_0_), channel_id=1, source_target_pairs={{0,6},{2,4},{4,2},{6,0},{8,14},{10,12},{12,10},{14,8},{16,22},{18,... | collective-permute-start | bytes 24584 | tf_op jit(solution)/shard_map/ppermute | solution.py:254
